TPU v7x, 8 devices: a whole 2x2x1 slice. The times are simulated.
8 devices in a mesh: m: 1 (over z), kk: 2 (over y), g: 4 (over x, core).
Axes of the slice: x: 2, y: 2, z: 1, core: 2. Of those that a mesh axis runs over, the one named last changes fastest.
Arguments:
- a_mat: bfloat16 [2, 8192, 28672], P(None, ('m', 'g'), 'kk')
Outputs:
- output: float32 [4, 3, 2, 2048, 2048], P(('m', 'g'))
All inputs are finite; a program needn't handle non-finite values.
Results may differ from a plain program's by a relative error of at most 0.001.
Values are sent between devices in bfloat16 or wider.
A program may use at most 1 GiB of HBM per device.

v0:
```python
import jax
import jax.numpy as jnp
from jax import lax
from jax.sharding import PartitionSpec as P


def assignment_table(groups):
    slot_count = groups // 2 + 1
    log_two = groups.bit_length() - 1
    side_len = 2 ** (log_two // 2)
    dup_count = groups // (side_len * side_len)
    grp_width = groups // side_len
    piece_len = max(1, grp_width // (2 * dup_count))
    pair_lists = [[] for device_no in range(groups)]
    block_sets = [set() for device_no in range(groups)]
    spill_pairs = []
    for upper_grp in range(side_len):
        for lower_grp in range(upper_grp):
            for left_row in range(upper_grp * grp_width, (upper_grp + 1) * grp_width):
                part_no = (left_row % grp_width) // piece_len
                if part_no < dup_count:
                    target = dup_count * (upper_grp * side_len + lower_grp) + part_no
                else:
                    target = dup_count * (lower_grp * side_len + upper_grp) + part_no - dup_count
                for right_row in range(lower_grp * grp_width, (lower_grp + 1) * grp_width):
                    pair_lists[target].append((left_row, right_row))
                    block_sets[target].update([left_row, right_row])
    for diag_grp in range(side_len):
        first_dev = dup_count * (diag_grp * side_len + diag_grp)
        for left_row in range(diag_grp * grp_width, (diag_grp + 1) * grp_width):
            for right_row in range(diag_grp * grp_width, left_row + 1):
                target = -1
                for copy_no in range(dup_count):
                    if target < 0 and len(pair_lists[first_dev + copy_no]) < slot_count:
                        target = first_dev + copy_no
                if target < 0:
                    spill_pairs.append((left_row, right_row))
                else:
                    pair_lists[target].append((left_row, right_row))
                    block_sets[target].update([left_row, right_row])
    for (left_row, right_row) in spill_pairs:
        best_score = (3, groups + 1, groups)
        for device_no in range(groups):
            if len(pair_lists[device_no]) < slot_count:
                growth = len(set([left_row, right_row]) - block_sets[device_no])
                cand_score = (growth, len(pair_lists[device_no]), device_no)
                best_score = min(best_score, cand_score)
        target = best_score[2]
        pair_lists[target].append((left_row, right_row))
        block_sets[target].update([left_row, right_row])
    return pair_lists, block_sets


def fetch_plan(groups):
    pair_lists, block_sets = assignment_table(groups)
    slot_count = groups // 2 + 1
    src_color = {}
    dst_color = {}
    for receiver in range(groups):
        for sender in sorted(block_sets[receiver]):
            if sender != receiver:
                color_a = 0
                while (sender, color_a) in src_color:
                    color_a += 1
                color_b = 0
                while (receiver, color_b) in dst_color:
                    color_b += 1
                if (receiver, color_a) in dst_color:
                    path_edges = []
                    node_no = receiver
                    wanted = color_a
                    at_receiver = True
                    found_node = dst_color.get((node_no, wanted))
                    while found_node is not None:
                        if at_receiver:
                            path_edges.append((found_node, node_no, wanted))
                        else:
                            path_edges.append((node_no, found_node, wanted))
                        node_no = found_node
                        at_receiver = not at_receiver
                        wanted = color_b if wanted == color_a else color_a
                        if at_receiver:
                            found_node = dst_color.get((node_no, wanted))
                        else:
                            found_node = src_color.get((node_no, wanted))
                    for (from_dev, to_dev, color_no) in path_edges:
                        src_color.pop((from_dev, color_no))
                        dst_color.pop((to_dev, color_no))
                    for (from_dev, to_dev, color_no) in path_edges:
                        new_color = color_b if color_no == color_a else color_a
                        src_color[(from_dev, new_color)] = to_dev
                        dst_color[(to_dev, new_color)] = from_dev
                src_color[(sender, color_a)] = receiver
                dst_color[(receiver, color_a)] = sender
    round_count = 1 + max([color_no for (node_no, color_no) in src_color])
    rounds = [sorted([(from_dev, to_dev) for ((from_dev, color_no), to_dev) in src_color.items() if color_no == round_no]) for round_no in range(round_count)]
    left_slot = []
    right_slot = []
    live_flags = []
    for device_no in range(groups):
        slot_map = {device_no: 0}
        for round_no in range(round_count):
            if (device_no, round_no) in dst_color:
                slot_map[dst_color[(device_no, round_no)]] = 1 + round_no
        own_pairs = pair_lists[device_no]
        left_slot.append([slot_map[own_pairs[slot_no][0]] if slot_no < len(own_pairs) else 0 for slot_no in range(slot_count)])
        right_slot.append([slot_map[own_pairs[slot_no][1]] if slot_no < len(own_pairs) else 0 for slot_no in range(slot_count)])
        live_flags.append([1 if slot_no < len(own_pairs) else 0 for slot_no in range(slot_count)])
    return rounds, left_slot, right_slot, live_flags


def solution(mesh):
    groups = mesh.shape["g"]
    rounds, left_slot, right_slot, live_flags = fetch_plan(groups)

    def local_part(a_loc):
        layer_count, block_rows, k_cols = a_loc.shape
        dev_index = lax.axis_index("g")
        received = [lax.ppermute(a_loc, "g", round_pairs) for round_pairs in rounds]
        held_blocks = jnp.stack([a_loc] + received, axis=0)
        left_slots = jnp.array(left_slot, jnp.int32)[dev_index]
        right_slots = jnp.array(right_slot, jnp.int32)[dev_index]
        live_slots = jnp.array(live_flags, jnp.int32)[dev_index]

        def one_slot(slot_args):
            left_no, right_no, live_flag = slot_args

            def compute():
                left_blk = lax.dynamic_index_in_dim(held_blocks, left_no, 0, keepdims=False)
                right_blk = lax.dynamic_index_in_dim(held_blocks, right_no, 0, keepdims=False)
                return jnp.einsum("lbk,lck->lbc", left_blk, right_blk, preferred_element_type=jnp.float32)

            def skip_slot():
                return jnp.zeros((layer_count, block_rows, block_rows), jnp.float32)

            return lax.cond(live_flag == 1, compute, skip_slot)

        partial_sums = lax.map(one_slot, (left_slots, right_slots, live_slots))
        totals = lax.psum(partial_sums, "kk")
        return totals[None]

    return jax.shard_map(local_part, mesh=mesh, in_specs=(P(None, ("m", "g"), "kk"),), out_specs=P(("m", "g"), None, None, None, None), check_vma=False)
```

profile of v0, /device:TPU:0, one launch (start us, length us, event | category | flops | bytes accessed | tf_op | source)
XLA Modules:
  0.0 5869.2 jit_solution(13870152713908639691)
XLA Ops:
  6.5 0.0 all-reduce.2.cloned.1.call-start
  6.5 38.5 collective-permute-start.1
  45.1 0.0 collective-permute-start
  45.1 1.2 fusion.13
  46.3 1.2 fusion.11
  47.5 130.5 %collective-permute-done.1 = bf16[2,2048,14336]{2,1,0:T(8,128)(2,1)} collective-permute-done((bf16[2,2048,14336]{2,1,0:T(8,128)(2,1)}, bf16[2,2048,14336]{2,1,0:T(8,128)(2,1)}, u32[]{:S(2)}, u32[]{:S(2)}) %collective-permute-start.1) | collective-permute-done | bytes 117440544 | tf_op jit(solution)/shard_map/ppermute | solution.py:119
  178.0 2350.9 %collective-permute-done = bf16[2,2048,14336]{2,1,0:T(8,128)(2,1)} collective-permute-done((bf16[2,2048,14336]{2,1,0:T(8,128)(2,1)}, bf16[2,2048,14336]{2,1,0:T(8,128)(2,1)}, u32[]{:S(2)}, u32[]{:S(2)}) %collective-permute-start) | collective-permute-done | bytes 117440544 | tf_op jit(solution)/shard_map/ppermute | solution.py:119
  2529.0 0.0 copy-start
  2529.0 0.0 copy-start.2
  2529.0 0.0 copy-start.3
  2529.0 229.2 %pad_maximum_fusion = bf16[3,2,2048,14336]{3,2,1,0:T(8,128)(2,1)} fusion(bf16[1,2,2048,14336]{3,2,1,0:T(8,128)(2,1)} %bitcast.10, bf16[1,2,2048,14336]{3,2,1,0:T(8,128)(2,1)} %bitcast.9, bf16[1,2,2048,14336]{3,2,1,0:T(8,128)(2,1)} %bitcast.8), kind=kLoop, calls=%fused_computation.8 | loop fusion | flops 352321536 | bytes 704643072 | tf_op jit(solution)/shard_map/stack | solution.py:120
  2758.2 0.0 copy-done
  2758.2 0.0 copy-done.2
  2758.2 0.0 copy-done.3
  2758.2 864.4 %while.10 = (s32[]{:T(128)}, f32[3,2,2048,2048]{3,2,1,0:T(8,128)}, s32[3]{0:T(128)S(1)}, s32[3]{0:T(128)S(1)}, bf16[3,2,2048,14336]{3,2,1,0:T(8,128)(2,1)}, /*in...) while((s32[]{:T(128)}, f32[3,2,2048,2048]{3,2,1,0:T(8,128)}, s32[3]{0:T(128)S(1)}, s32[3]{0:T(128)S(1)}, ...), condition=%wide.region_3.4_spmd, body=%wide.region_0.3_spmd.sunk | while | flops 240518168576 | bytes 335545120 | solution.py:138
  2758.3 0.6 dynamic_slice.63
  2759.5 0.0 copy-start.1
  2759.5 263.7 %conditional.2 = (f32[1,2,2048,2048]{3,2,1,0:T(8,128)}) conditional(s32[]{:T(128)} %bitcast.34, () %tuple.31, (s32[3]{0:T(128)S(1)}, s32[]{:T(128)}, bf16[3,2,2048,14336]{3,2,1,0:T(8,128)(2,1)}, s32[3]{0:T(128)S(1)}) %tuple.32), branch_computations={%region_1.1_spmd, %region_2.2_spmd} | conditional | flops 240518168576 | bytes 268435552 | solution.py:136
  2759.5 0.6 dynamic_slice.24
  2762.0 0.6 dynamic_slice.26
  2764.4 258.8 %fusion.5 = f32[1,2,2048,2048]{3,2,1,0:T(8,128)} fusion(bf16[3,2,2048,14336]{3,2,1,0:T(8,128)(2,1)} %get-tuple-element.55, s32[]{:T(128)S(6)} %select_n.12, s32[]{:T(128)S(6)} %select_n.11), kind=kOutput, calls=%fused_computation.5 | convolution fusion | flops 240518168576 | bytes 268435456 | tf_op jit(solution)/shard_map/while/body/eval_jaxpr/cond/branch_1_fun/lbk,lck->lbc/dot_general | solution.py:131
  3023.2 23.2 constant_dynamic-update-slice_fusion.2
  3046.4 0.0 copy-done.1
  3046.4 0.6 dynamic_slice.63
  3047.6 0.0 copy-start.1
  3047.6 263.7 %conditional.2 = (f32[1,2,2048,2048]{3,2,1,0:T(8,128)}) conditional(s32[]{:T(128)} %bitcast.34, () %tuple.31, (s32[3]{0:T(128)S(1)}, s32[]{:T(128)}, bf16[3,2,2048,14336]{3,2,1,0:T(8,128)(2,1)}, s32[3]{0:T(128)S(1)}) %tuple.32), branch_computations={%region_1.1_spmd, %region_2.2_spmd} | conditional | flops 240518168576 | bytes 268435552 | solution.py:136
  3047.6 0.6 dynamic_slice.24
  3050.1 0.6 dynamic_slice.26
  3052.5 258.8 %fusion.5 = f32[1,2,2048,2048]{3,2,1,0:T(8,128)} fusion(bf16[3,2,2048,14336]{3,2,1,0:T(8,128)(2,1)} %get-tuple-element.55, s32[]{:T(128)S(6)} %select_n.12, s32[]{:T(128)S(6)} %select_n.11), kind=kOutput, calls=%fused_computation.5 | convolution fusion | flops 240518168576 | bytes 268435456 | tf_op jit(solution)/shard_map/while/body/eval_jaxpr/cond/branch_1_fun/lbk,lck->lbc/dot_general | solution.py:131
  3311.4 23.2 constant_dynamic-update-slice_fusion.2
  3334.5 0.0 copy-done.1
  3334.5 0.6 dynamic_slice.63
  3335.7 0.0 copy-start.1
  3335.7 263.7 %conditional.2 = (f32[1,2,2048,2048]{3,2,1,0:T(8,128)}) conditional(s32[]{:T(128)} %bitcast.34, () %tuple.31, (s32[3]{0:T(128)S(1)}, s32[]{:T(128)}, bf16[3,2,2048,14336]{3,2,1,0:T(8,128)(2,1)}, s32[3]{0:T(128)S(1)}) %tuple.32), branch_computations={%region_1.1_spmd, %region_2.2_spmd} | conditional | flops 240518168576 | bytes 268435552 | solution.py:136
  3335.8 0.6 dynamic_slice.24
  3338.2 0.6 dynamic_slice.26
  3340.7 258.8 %fusion.5 = f32[1,2,2048,2048]{3,2,1,0:T(8,128)} fusion(bf16[3,2,2048,14336]{3,2,1,0:T(8,128)(2,1)} %get-tuple-element.55, s32[]{:T(128)S(6)} %select_n.12, s32[]{:T(128)S(6)} %select_n.11), kind=kOutput, calls=%fused_computation.5 | convolution fusion | flops 240518168576 | bytes 268435456 | tf_op jit(solution)/shard_map/while/body/eval_jaxpr/cond/branch_1_fun/lbk,lck->lbc/dot_general | solution.py:131
  3599.5 23.2 constant_dynamic-update-slice_fusion.2
  3622.6 0.0 copy-done.1
  3622.6 0.0 all-reduce.2.cloned.1.call-update
  3622.7 2174.3 %all-reduce.2.cloned.1.call-done = f32[1,3,2,2048,2048]{4,3,2,1,0:T(8,128)} async-done(((f32[1,3,2,2048,2048]{4,3,2,1,0:T(8,128)}), f32[1,3,2,2048,2048]{4,3,2,1,0:T(8,128)}) %all-reduce.2.cloned.1.call-update) | async-done | bytes 100663312 | tf_op jit(solution)/shard_map/psum | solution.py:139
  5796.9 65.4 %copy.17 = f32[1,3,2,2048,2048]{4,3,2,1,0:T(8,128)} copy(f32[1,3,2,2048,2048]{4,3,2,1,0:T(8,128)} %all-reduce.2.cloned.1.call-done) | data formatting | bytes 201326592
  (1 shorter events, 0.0 us)
Async XLA Ops:
  6.5 5790.4 %all-reduce.2.cloned.1.call-start = ((), (), s32[]{:S(2)}) async-start(), calls=%async_computation | async-start | bytes 201326592 | tf_op jit(solution)/shard_map/psum | solution.py:139
  6.5 171.5 %collective-permute-start.1 = (bf16[2,2048,14336]{2,1,0:T(8,128)(2,1)}, bf16[2,2048,14336]{2,1,0:T(8,128)(2,1)}, u32[]{:S(2)}, u32[]{:S(2)}) collective-permute-start(bf16[2,2048,14336]{2,1,0:T(8,128)(2,1)} %param.8), channel_id=1, source_target_pairs={{0,1},{1,2},{4,5},{5,6}} | collective-permute-start | bytes 352321536 | tf_op jit(solution)/shard_map/ppermute | solution.py:119
  45.1 2483.9 %collective-permute-start = (bf16[2,2048,14336]{2,1,0:T(8,128)(2,1)}, bf16[2,2048,14336]{2,1,0:T(8,128)(2,1)}, u32[]{:S(2)}, u32[]{:S(2)}) collective-permute-start(bf16[2,2048,14336]{2,1,0:T(8,128)(2,1)} %param.8), channel_id=1, source_target_pairs={{0,2},{1,0},{2,3},{3,1},{4,6},{5,4},{6,7},{7,5}} | collective-permute-start | bytes 352321536 | tf_op jit(solution)/shard_map/ppermute | solution.py:119
  2529.0 229.2 %copy-start = (s32[3]{0:T(128)S(1)}, s32[3]{0:T(128)}, u32[]{:S(2)}) copy-start(s32[3]{0:T(128)} %get-tuple-element.121) | copy-start | bytes 40
  2529.0 229.3 %copy-start.2 = (s32[3]{0:T(128)S(1)}, s32[3]{0:T(128)}, u32[]{:S(2)}) copy-start(s32[3]{0:T(128)} %get-tuple-element.122) | copy-start | bytes 40
  2529.0 229.3 %copy-start.3 = (s32[3]{0:T(128)S(1)}, s32[3]{0:T(128)}, u32[]{:S(2)}) copy-start(s32[3]{0:T(128)} %fusion.13) | copy-start | bytes 40
  2759.5 286.9 %copy-start.1 = (s32[3]{0:T(128)S(1)}, s32[3]{0:T(128)}, u32[]{:S(2)}) copy-start(s32[3]{0:T(128)} %get-tuple-element.153) | copy-start | bytes 40 | tf_op jit(solution)/shard_map/while
  3047.6 286.9 %copy-start.1 = (s32[3]{0:T(128)S(1)}, s32[3]{0:T(128)}, u32[]{:S(2)}) copy-start(s32[3]{0:T(128)} %get-tuple-element.153) | copy-start | bytes 40 | tf_op jit(solution)/shard_map/while
  3335.7 286.9 %copy-start.1 = (s32[3]{0:T(128)S(1)}, s32[3]{0:T(128)}, u32[]{:S(2)}) copy-start(s32[3]{0:T(128)} %get-tuple-element.153) | copy-start | bytes 40 | tf_op jit(solution)/shard_map/while
Sparse Core Ops, SparseCore 0:
  3622.8 2174.1 all-reduce.1
where the time goes:
time: 5870 us
  waiting for transfers between devices  4660 us (79%)
  matrix products  776 us (13%)
  other arithmetic  229 us (4%)
  local copies, waits for them, and re-layouts  143 us (2%)
    ppermute x2, waiting for transfers between devices, local_part(): received = [lax.ppermute(a_loc, 'g', round_pairs) for round_pairs in rounds]  2480 us
    psum x1, waiting for transfers between devices, local_part(): totals = lax.psum(partial_sums, 'kk')  2170 us
    dot_general x3, matrix products, compute(): jnp.einsum('lbk,lck->lbc', left_blk, right_blk, preferred_element_type=jn...  776 us
    another operation x1, other arithmetic, local_part(): held_blocks = jnp.stack([a_loc] + received, axis=0)  229 us
  transfers between devices with their start and end apart: 3, of which 3 were waited for; matrix products, arithmetic and copies ran while one was open for 0% of the time, Pallas kernels for 0%

commit v1 on v0

v1 whole, which is shorter than its diff:
```python
import jax
import jax.numpy as jnp
from jax import lax
from jax.experimental import pallas as pl
from jax.experimental.pallas import tpu as pltpu
from jax.sharding import PartitionSpec as P

MESH = pl.DeviceIdType.MESH
NT = (((1,), (1,)), ((), ()))
F32 = jnp.float32

TILE = 512
CHUNK = 128
STRIPS = 24
KSTEPS = 2


def kernel(a, out, blk, prv, awy, res, stm, acc, fa, fb, fc,
           s_x, r_x, s_d, r_d, s_y, r_y, s_r, r_r,
           l_res, l_stm, l_acc, l_fa, l_fb, l_st, l_tr):
    m = lax.axis_index("m")
    y = lax.axis_index("kk")
    g = lax.axis_index("g")
    side = lax.div(g, 2)
    layers, rows, cols = a.shape
    kc = cols // KSTEPS
    n_strip = rows // TILE
    n_chunk = rows // CHUNK

    def at(start, size):
        return pl.ds(pl.multiple_of(start, size), size)

    def remote(src, dst, ss, rs, kk2, g2):
        return pltpu.make_async_remote_copy(src, dst, ss, rs, device_id=(m, kk2, g2), device_id_type=MESH)

    barrier = pltpu.get_barrier_semaphore()
    me = y * 4 + g
    for step in range(1, 8):
        other = lax.rem(me + step, 8)
        pl.semaphore_signal(barrier, inc=1, device_id=(m, lax.div(other, 4), lax.rem(other, 4)), device_id_type=MESH)
    pl.semaphore_wait(barrier, 7)

    def x_in(c):
        part = lax.rem(g, 2)
        return remote(a.at[1 - side, at(c * CHUNK, CHUNK)], blk.at[1 + part, at(c * CHUNK, CHUNK)],
                      s_x.at[c], r_x.at[part, c], y, 2 - side)

    def x_start(c, carry):
        x_in(c).start()
        return carry

    def x_wait_send(c, carry):
        x_in(c).wait_send()
        return carry

    def body_steps(res_view, acc_view, swap, after):
        acc_view[...] = jnp.zeros(acc_view.shape, F32)

        def step(k, carry):
            pltpu.make_async_copy(a.at[0, pl.ds(0, TILE), pl.ds(0, kc)], stm.at[k], l_stm.at[k]).wait()
            lhs = res_view[:, at(k * kc, kc)]
            rhs = stm[k]
            if swap:
                lhs, rhs = rhs, lhs
            acc_view[...] += lax.dot_general(lhs, rhs, NT, preferred_element_type=F32)
            after(k)
            return carry

        lax.fori_loop(0, KSTEPS, step, 0)

    def diagonal():
        d = lax.div(g, 3)
        mate = g + 1 - 2 * d
        d2d = remote(a.at[side], blk.at[0], s_d.at[0], r_d.at[0], y, mate)
        d2d.start()
        lax.fori_loop(0, n_chunk, x_start, 0)

        def phase(r):
            return lax.div(r, 8), lax.rem(lax.div(r, 4), 2), lax.rem(r, 4)

        def count(r):
            p, _, i = phase(r)
            return (i + 1) + lax.rem(p, 2) * (n_strip - 1 - i)

        def slot(p):
            return p * (1 - 2 * d) + 2 * d

        def load(own, layer, row, col, width, dst, sem):
            @pl.when(own)
            def _():
                pltpu.make_async_copy(a.at[layer, at(row, TILE), at(col, width)], dst, sem).start()

            @pl.when(jnp.logical_not(own))
            def _():
                pltpu.make_async_copy(blk.at[layer, at(row, TILE), at(col, width)], dst, sem).start()

        def load_res(r):
            p, layer, i = phase(r)
            own = p + 1 - d < 2
            load(own, layer, i * TILE, 0, cols, res.at[lax.rem(r, 2)], l_res.at[lax.rem(r, 2)])

        def load_stm(r, j, k):
            p, layer, _ = phase(r)
            own = p + d < 2
            load(own, layer, j * TILE, k * kc, kc, stm.at[k], l_stm.at[k])

        def tile_of(ref, r, i, j):
            p, layer, _ = phase(r)
            return ref.at[slot(p), layer, at(i * TILE, TILE), at(j * TILE, TILE)]

        def is_diag(r, j):
            p, _, i = phase(r)
            return jnp.logical_and(p != 1, i == j)

        def is_mirror(r, j):
            p, _, i = phase(r)
            return jnp.logical_and(p != 1, i != j)

        def whole(r, j):
            i = lax.rem(r, 4)
            return remote(tile_of(out, r, i, j), tile_of(prv, r, i, j),
                          s_y.at[lax.rem(r, 4) * 4 + j], r_y.at[r * 4 + j], 1 - y, g)

        def lower(r, j, row, height, width):
            p, layer, i = phase(r)

            def part(ref):
                return ref.at[slot(p), layer, pl.ds(pl.multiple_of(i * TILE + row, 128), height), pl.ds(pl.multiple_of(j * TILE, TILE), width)]

            return remote(part(out), part(prv), s_y.at[lax.rem(r, 4) * 4 + j], r_y.at[r * 4 + j], 1 - y, g)

        def send(r, j):
            @pl.when(is_diag(r, j))
            def _():
                for q in range(4):
                    lower(r, j, q * 128, 128, (q + 1) * 128).start()

            @pl.when(jnp.logical_not(is_diag(r, j)))
            def _():
                whole(r, j).start()

        def wait_exchange(r, j):
            @pl.when(is_diag(r, j))
            def _():
                sized = lower(r, j, 0, 320, TILE)
                sized.wait_send()
                sized.wait_recv()

            @pl.when(jnp.logical_not(is_diag(r, j)))
            def _():
                whole(r, j).wait_send()
                whole(r, j).wait_recv()

        def store_acc(r, j):
            return pltpu.make_async_copy(acc.at[lax.rem(j, 2)], tile_of(out, r, lax.rem(r, 4), j), l_acc.at[lax.rem(j, 2)])

        def finish(r):
            n = count(r)
            i = lax.rem(r, 4)

            def loads(j):
                b = lax.rem(j, 2)
                return (pltpu.make_async_copy(tile_of(out, r, i, j), fa.at[b], l_fa.at[b]),
                        pltpu.make_async_copy(tile_of(prv, r, i, j), fb.at[b], l_fb.at[b]))

            def start_loads(j):
                wait_exchange(r, j)
                for copy in loads(j):
                    copy.start()

            def main_store(j):
                return pltpu.make_async_copy(fa.at[lax.rem(j, 2)], tile_of(out, r, i, j), l_st.at[lax.rem(j, 2)])

            def mirror_store(j):
                return pltpu.make_async_copy(fc.at[lax.rem(j, 2)], tile_of(out, r, j, i), l_tr.at[lax.rem(j, 2)])

            def wait_stores(j):
                main_store(j).wait()

                @pl.when(is_mirror(r, j))
                def _():
                    mirror_store(j).wait()

            start_loads(0)

            def one(j, carry):
                b = lax.rem(j, 2)

                @pl.when(j + 1 < n)
                def _():
                    @pl.when(j >= 1)
                    def _():
                        wait_stores(j - 1)

                    start_loads(j + 1)

                for copy in loads(j):
                    copy.wait()
                fa[b] = fa[b] + fb[b]

                @pl.when(is_mirror(r, j))
                def _():
                    fc[b] = fa[b].T
                    mirror_store(j).start()

                @pl.when(is_diag(r, j))
                def _():
                    total = fa[b]
                    at_row = lax.broadcasted_iota(jnp.int32, (TILE, TILE), 0)
                    at_col = lax.broadcasted_iota(jnp.int32, (TILE, TILE), 1)
                    fa[b] = jnp.where(at_row >= at_col, total, total.T)

                main_store(j).start()
                return carry

            lax.fori_loop(0, n, one, 0)

            @pl.when(n >= 2)
            def _():
                wait_stores(n - 2)

            wait_stores(n - 1)

        load_res(0)
        for k in range(KSTEPS):
            load_stm(0, 0, k)

        def strip(r, carry):
            @pl.when(r == 7)
            def _():
                remote(a.at[0], blk.at[0], s_d.at[0], r_d.at[0], y, mate).wait_recv()

            @pl.when(r == 11)
            def _():
                remote(a.at[1], blk.at[1], s_d.at[1], r_d.at[1], y, mate).wait_recv()

            @pl.when(r + 1 < STRIPS)
            def _():
                load_res(r + 1)

            pltpu.make_async_copy(a.at[0, pl.ds(0, TILE)], res.at[lax.rem(r, 2)], l_res.at[lax.rem(r, 2)]).wait()
            n = count(r)

            def tile(j, carry):
                last = lax.div(j + 1, n)

                def after(k):
                    @pl.when(r + last < STRIPS)
                    def _():
                        load_stm(r + last, (j + 1) * (1 - last), k)

                    @pl.when(jnp.logical_and(k == 0, j >= 1))
                    def _():
                        store_acc(r, j - 1).wait()
                        send(r, j - 1)

                body_steps(res.at[lax.rem(r, 2)], acc.at[lax.rem(j, 2)], False, after)
                store_acc(r, j).start()
                return carry

            lax.fori_loop(0, n, tile, 0)
            store_acc(r, n - 1).wait()
            send(r, n - 1)

            @pl.when(r >= 2)
            def _():
                finish(r - 2)

            return carry

        lax.fori_loop(0, STRIPS, strip, 0)
        lax.fori_loop(STRIPS - 2, STRIPS, lambda r, carry: (finish(r), carry)[1], 0)
        d2d.wait_send()
        lax.fori_loop(0, n_chunk, x_wait_send, 0)

    def cross(is_left):
        lc = 0 if is_left else 1
        mate = 0 if is_left else 3
        partner = 2 if is_left else 1
        for layer in range(layers):
            remote(a.at[layer], blk.at[layer], s_d.at[layer], r_d.at[layer], y, mate).start()
        lax.fori_loop(0, n_chunk, x_start, 0)

        fc[0] = jnp.zeros((TILE, TILE), F32)

        def zero(t, carry):
            copies = [pltpu.make_async_copy(fc.at[0], out.at[2, lax.div(t, 4), at(lax.rem(t, 4) * TILE, TILE), pl.ds(q * TILE, TILE)], l_fa.at[q])
                      for q in range(4)]
            for copy in copies:
                copy.start()
            for copy in copies:
                copy.wait()
            return carry

        lax.fori_loop(0, layers * n_strip, zero, 0)
        remote(a.at[lc], blk.at[0], s_d.at[0], r_d.at[0], y, mate).wait_recv()

        def region(ref, rows_first, c):
            return ref.at[at(c * CHUNK, CHUNK), :] if rows_first else ref.at[:, at(c * CHUNK, CHUNK)]

        def piece(ref, c, q):
            if is_left:
                return ref.at[at(c * CHUNK, CHUNK), at(q * TILE, TILE)]
            return ref.at[at(q * TILE, TILE), at(c * CHUNK, CHUNK)]

        def block_of(half):
            return lax.rem(half + 1 - y + 2, 2)

        def kept(b):
            return lax.rem(b + 1 - y + 2, 2)

        def load_stm(t, k):
            half, js = lax.div(t, 4), lax.rem(t, 4)
            own = block_of(half) == 1 if is_left else half == 1

            @pl.when(own)
            def _():
                pltpu.make_async_copy(a.at[lc, at(js * TILE, TILE), at(k * kc, kc)], stm.at[k], l_stm.at[k]).start()

            @pl.when(jnp.logical_not(own))
            def _():
                pltpu.make_async_copy(blk.at[0, at(js * TILE, TILE), at(k * kc, kc)], stm.at[k], l_stm.at[k]).start()

        def res_copy(c, part):
            b = lax.rem(c, 2)
            return pltpu.make_async_copy(blk.at[1 + part, at(c * CHUNK, CHUNK)], res.at[b, pl.ds(part * CHUNK, CHUNK)], l_fb.at[part])

        def acc_view(t):
            b = lax.rem(t, 2)
            return acc.at[b, pl.ds(0, 2 * CHUNK), :] if is_left else acc.at[b, :, pl.ds(0, 2 * CHUNK)]

        def store_acc(c, t):
            b, half, js = lax.rem(t, 2), lax.div(t, 4), lax.rem(t, 4)

            def views(q, dst):
                src = acc.at[b, pl.ds(q * CHUNK, CHUNK), :] if is_left else acc.at[b, :, pl.ds(q * CHUNK, CHUNK)]
                return pltpu.make_async_copy(src, piece(dst, c, js), l_acc.at[b * 2 + q])

            if is_left:
                return lambda op: (op(views(0, awy.at[half])), op(views(1, out.at[block_of(half), lc])))

            def both(op):
                @pl.when(half == 0)
                def _():
                    for q in range(2):
                        op(views(q, awy.at[kept(q)]))

                @pl.when(half == 1)
                def _():
                    for q in range(2):
                        op(views(q, out.at[q, lc]))

            return both

        def home(c, b):
            return remote(region(out.at[b, lc], is_left, c), region(prv.at[b, lc], is_left, c),
                          s_y.at[c * 2 + b], r_y.at[c * 2 + b], 1 - y, g)

        def spread(c):
            return remote(region(awy.at[0], is_left, c), region(prv.at[2, 0], is_left, c),
                          s_y.at[2 * n_chunk + c], r_y.at[2 * n_chunk + c], 1 - y, g)

        def away(c):
            return remote(region(awy.at[1], is_left, c), region(out.at[y, lc], is_left, c),
                          s_r.at[c], r_r.at[c], y, partner)

        def arrived(c):
            return remote(region(awy.at[1], not is_left, c), region(out.at[y, 1 - lc], not is_left, c),
                          s_r.at[c], r_r.at[c], y, partner)

        def gather(c, owner):
            here = region(out.at[owner, 1 - lc], not is_left, c)
            return remote(here, here, s_y.at[3 * n_chunk + c], r_y.at[3 * n_chunk + c], 1 - y, g)

        def add(c, local, received):
            def view(ref, q):
                return ref.at[0, pl.ds(q * CHUNK, CHUNK), :] if is_left else ref.at[0, :, pl.ds(q * CHUNK, CHUNK)]

            pairs = [(pltpu.make_async_copy(piece(local, c, q), view(fa, q), l_fa.at[q]),
                      pltpu.make_async_copy(piece(received, c, q), view(fb, q), l_fb.at[q])) for q in range(4)]
            for pair in pairs:
                for copy in pair:
                    copy.start()
            stores = [pltpu.make_async_copy(view(fa, q), piece(local, c, q), l_st.at[q]) for q in range(4)]
            for q in range(4):
                for copy in pairs[q]:
                    copy.wait()
                view(fa, q)[...] = view(fa, q)[...] + view(fb, q)[...]
                stores[q].start()
            for q in range(4):
                stores[q].wait()

        def finish_away(c):
            spread(c).wait_recv()
            add(c, awy.at[1], prv.at[2, 0])
            away(c).start()

        def finish_home(c):
            for b in range(2):
                home(c, b).wait_send()
                home(c, b).wait_recv()
                add(c, out.at[b, lc], prv.at[b, lc])

        def forward(c):
            arrived(c).wait_recv()
            gather(c, y).start()

        for k in range(KSTEPS):
            load_stm(0, k)

        def compute(c):
            for part in range(2):
                remote(a.at[0, pl.ds(0, CHUNK)], blk.at[1 + part, at(c * CHUNK, CHUNK)], s_x.at[0], r_x.at[part, c], y, partner).wait_recv()
                res_copy(c, part).start()
            for part in range(2):
                res_copy(c, part).wait()

            def send_half(half):
                if is_left:
                    @pl.when(half == 0)
                    def _():
                        spread(c).start()

                    home(c, block_of(half)).start()
                else:
                    @pl.when(half == 0)
                    def _():
                        spread(c).start()

                    @pl.when(half == 1)
                    def _():
                        for b in range(2):
                            home(c, b).start()

            def tile(t, carry):
                last = lax.div(t + 1, 8)

                def after(k):
                    @pl.when(c + last < n_chunk)
                    def _():
                        load_stm((t + 1) * (1 - last), k)

                    @pl.when(jnp.logical_and(k == 0, t >= 1))
                    def _():
                        store_acc(c, t - 1)(lambda copy: copy.wait())

                        @pl.when(t == 4)
                        def _():
                            send_half(0 * t)

                body_steps(res.at[lax.rem(c, 2), pl.ds(0, 2 * CHUNK), :], acc_view(t), not is_left, after)
                store_acc(c, t)(lambda copy: copy.start())
                return carry

            lax.fori_loop(0, 8, tile, 0)
            store_acc(c, 7)(lambda copy: copy.wait())
            send_half(1 + 0 * c)

        def chunk(c, carry):
            compute(c)

            @pl.when(c >= 1)
            def _():
                finish_away(c - 1)
                finish_home(c - 1)

            return carry

        def forwards(first, stop):
            lax.fori_loop(first, stop, lambda c, carry: (forward(c), carry)[1], 0)

        lax.fori_loop(0, n_chunk, chunk, 0)
        end = n_chunk - 1
        forwards(0, n_chunk // 4)
        finish_away(end)
        forwards(n_chunk // 4, 5 * n_chunk // 8)
        finish_home(end)
        forwards(5 * n_chunk // 8, n_chunk)

        def drain(c, carry):
            spread(c).wait_send()
            away(c).wait_send()
            gather(c, y).wait_send()
            gather(c, 1 - y).wait_recv()
            return carry

        lax.fori_loop(0, n_chunk, drain, 0)
        for layer in range(layers):
            remote(a.at[layer], blk.at[layer], s_d.at[layer], r_d.at[layer], y, mate).wait_send()
        lax.fori_loop(0, n_chunk, x_wait_send, 0)

    pl.when(lax.rem(g, 3) == 0)(diagonal)
    pl.when(g == 1)(lambda: cross(True))
    pl.when(g == 2)(lambda: cross(False))


def solution(mesh):
    assert dict(mesh.shape) == {"m": 1, "kk": 2, "g": 4}
    dma = pltpu.SemaphoreType.DMA

    def local_part(a_loc):
        layers, rows, cols = a_loc.shape
        n_chunk = rows // CHUNK
        any_space = pl.BlockSpec(memory_space=pl.ANY)
        result = pl.pallas_call(
            kernel,
            out_shape=(
                jax.ShapeDtypeStruct((3, layers, rows, rows), F32),
                jax.ShapeDtypeStruct((3, rows, cols), a_loc.dtype),
                jax.ShapeDtypeStruct((3, layers, rows, rows), F32),
                jax.ShapeDtypeStruct((2, rows, rows), F32),
            ),
            in_specs=[any_space],
            out_specs=(any_space,) * 4,
            scratch_shapes=[
                pltpu.VMEM((2, TILE, cols), a_loc.dtype),
                pltpu.VMEM((KSTEPS, TILE, cols // KSTEPS), a_loc.dtype),
                pltpu.VMEM((2, TILE, TILE), F32),
                pltpu.VMEM((2, TILE, TILE), F32),
                pltpu.VMEM((2, TILE, TILE), F32),
                pltpu.VMEM((2, TILE, TILE), F32),
                dma((n_chunk,)), dma((2, n_chunk)), dma((2,)), dma((2,)),
                dma((4 * n_chunk,)), dma((4 * STRIPS,)), dma((n_chunk,)), dma((n_chunk,)),
                dma((2,)), dma((KSTEPS,)), dma((4,)), dma((4,)), dma((4,)), dma((4,)), dma((2,)),
            ],
            compiler_params=pltpu.CompilerParams(
                collective_id=0, has_side_effects=True, vmem_limit_bytes=63 * 2**20),
            cost_estimate=pl.CostEstimate(flops=10**12, bytes_accessed=10**9, transcendentals=0),
        )(a_loc)
        return result[0][None]

    return jax.shard_map(local_part, mesh=mesh, in_specs=(P(None, ("m", "g"), "kk"),),
                         out_specs=P(("m", "g"), None, None, None, None), check_vma=False)
```

time: 5870 us -> 1590 us (0.27)
  the two profiles are of different devices: /device:TPU:0 before, /device:TPU:2 now
where the time goes in v1:
time: 1590 us; the launch traced here: 1580 us
  Pallas kernels  1520 us (96%)
  local copies, waits for them, and re-layouts  64.7 us (4%)
    pallas_call x1, Pallas kernels, local_part(): pl.pallas_call(kernel, out_shape=(jax.ShapeDtypeStruct((3, layers, rows,...  1520 us
    unnamed x1, local copies, waits for them, and re-layouts  64.7 us

profile of v1, /device:TPU:2, one launch (start us, length us, event | category | flops | bytes accessed | tf_op | source)
XLA Modules:
  0.0 1580.2 jit_solution(1487138759337218691)
XLA Ops:
  0.0 1515.5 %shard_map.17 = (f32[3,2,2048,2048]{3,2,1,0:T(8,128)}, bf16[3,2048,14336]{2,1,0:T(8,128)(2,1)}, f32[3,2,2048,2048]{3,2,1,0:T(8,128)}, f32[2,2048,2048]{2,1,0:T(8,128)}) custom-call(bf16[2,2048,14336]{2,1,0:T(8,128)(2,1)} %a.1), custom_call_target="tpu_custom_call" | custom-call | flops 999999995904 | bytes 1000000000 | tf_op jit(solution)/shard_map/pallas_call | solution.py:505
  1515.5 64.7 %copy.3 = f32[1,3,2,2048,2048]{4,3,2,1,0:T(8,128)} copy(f32[1,3,2,2048,2048]{4,3,2,1,0:T(8,128)} %bitcast) | data formatting | bytes 201326592

commit v2 on v1

--- a/solution.py
+++ b/solution.py
@@ -5,6 +5,7 @@
 from jax.experimental.pallas import tpu as pltpu
 from jax.sharding import PartitionSpec as P
 
+
 MESH = pl.DeviceIdType.MESH
 NT = (((1,), (1,)), ((), ()))
 F32 = jnp.float32
@@ -13,9 +14,17 @@
 CHUNK = 128
 STRIPS = 24
 KSTEPS = 2
-
-
-def kernel(a, out, blk, prv, awy, res, stm, acc, fa, fb, fc,
+LAG = 4
+INSIDE = 5
+PIECES = ((5, 6), (6, 7), (7, 9), (9, 11), (11, 13), (13, 15), (15, 16))
+
+
+def kernel(a, out, blk, prv, awy, late, *refs):
+    pieces, refs = refs[:len(PIECES)], refs[len(PIECES):]
+    work(a, out, blk, prv, awy, late, pieces, *refs)
+
+
+def work(a, out, blk, prv, awy, late, pieces, res, stm, acc, fa, fb, fc,
            s_x, r_x, s_d, r_d, s_y, r_y, s_r, r_r,
            l_res, l_stm, l_acc, l_fa, l_fb, l_st, l_tr):
     m = lax.axis_index("m")
@@ -53,10 +62,11 @@
         x_in(c).wait_send()
         return carry
 
-    def body_steps(res_view, acc_view, swap, after):
+    def body_steps(res_view, acc_view, swap, before, after):
         acc_view[...] = jnp.zeros(acc_view.shape, F32)
 
         def step(k, carry):
+            before(k)
             pltpu.make_async_copy(a.at[0, pl.ds(0, TILE), pl.ds(0, kc)], stm.at[k], l_stm.at[k]).wait()
             lhs = res_view[:, at(k * kc, kc)]
             rhs = stm[k]
@@ -72,11 +82,9 @@
         d = lax.div(g, 3)
         mate = g + 1 - 2 * d
         d2d = remote(a.at[side], blk.at[0], s_d.at[0], r_d.at[0], y, mate)
-        d2d.start()
-        lax.fori_loop(0, n_chunk, x_start, 0)
 
         def phase(r):
-            return lax.div(r, 8), lax.rem(lax.div(r, 4), 2), lax.rem(r, 4)
+            return lax.div(r, 8), lax.rem(lax.div(r, 4), 2), n_strip - 1 - lax.rem(r, 4)
 
         def count(r):
             p, _, i = phase(r)
@@ -94,10 +102,10 @@
             def _():
                 pltpu.make_async_copy(blk.at[layer, at(row, TILE), at(col, width)], dst, sem).start()
 
-        def load_res(r):
+        def load_res(r, k):
             p, layer, i = phase(r)
             own = p + 1 - d < 2
-            load(own, layer, i * TILE, 0, cols, res.at[lax.rem(r, 2)], l_res.at[lax.rem(r, 2)])
+            load(own, layer, i * TILE, k * kc, kc, res.at[lax.rem(r, 2), :, at(k * kc, kc)], l_res.at[lax.rem(r, 2) * KSTEPS + k])
 
         def load_stm(r, j, k):
             p, layer, _ = phase(r)
@@ -117,9 +125,9 @@
             return jnp.logical_and(p != 1, i != j)
 
         def whole(r, j):
-            i = lax.rem(r, 4)
+            i = phase(r)[2]
             return remote(tile_of(out, r, i, j), tile_of(prv, r, i, j),
-                          s_y.at[lax.rem(r, 4) * 4 + j], r_y.at[r * 4 + j], 1 - y, g)
+                          s_y.at[lax.rem(r, 8) * 4 + j], r_y.at[r * 4 + j], 1 - y, g)
 
         def lower(r, j, row, height, width):
             p, layer, i = phase(r)
@@ -127,7 +135,7 @@
             def part(ref):
                 return ref.at[slot(p), layer, pl.ds(pl.multiple_of(i * TILE + row, 128), height), pl.ds(pl.multiple_of(j * TILE, TILE), width)]
 
-            return remote(part(out), part(prv), s_y.at[lax.rem(r, 4) * 4 + j], r_y.at[r * 4 + j], 1 - y, g)
+            return remote(part(out), part(prv), s_y.at[lax.rem(r, 8) * 4 + j], r_y.at[r * 4 + j], 1 - y, g)
 
         def send(r, j):
             @pl.when(is_diag(r, j))
@@ -152,11 +160,11 @@
                 whole(r, j).wait_recv()
 
         def store_acc(r, j):
-            return pltpu.make_async_copy(acc.at[lax.rem(j, 2)], tile_of(out, r, lax.rem(r, 4), j), l_acc.at[lax.rem(j, 2)])
+            return pltpu.make_async_copy(acc.at[lax.rem(j, 2)], tile_of(out, r, phase(r)[2], j), l_acc.at[lax.rem(j, 2)])
 
         def finish(r):
             n = count(r)
-            i = lax.rem(r, 4)
+            i = phase(r)[2]
 
             def loads(j):
                 b = lax.rem(j, 2)
@@ -221,9 +229,11 @@
 
             wait_stores(n - 1)
 
-        load_res(0)
         for k in range(KSTEPS):
+            load_res(0, k)
             load_stm(0, 0, k)
+        d2d.start()
+        lax.fori_loop(0, n_chunk, x_start, 0)
 
         def strip(r, carry):
             @pl.when(r == 7)
@@ -234,17 +244,27 @@
             def _():
                 remote(a.at[1], blk.at[1], s_d.at[1], r_d.at[1], y, mate).wait_recv()
 
-            @pl.when(r + 1 < STRIPS)
-            def _():
-                load_res(r + 1)
-
-            pltpu.make_async_copy(a.at[0, pl.ds(0, TILE)], res.at[lax.rem(r, 2)], l_res.at[lax.rem(r, 2)]).wait()
+            @pl.when(jnp.logical_and(r >= 1, r + 1 < STRIPS))
+            def _():
+                for k in range(KSTEPS):
+                    load_res(r + 1, k)
+
             n = count(r)
 
             def tile(j, carry):
                 last = lax.div(j + 1, n)
 
+                def before(k):
+                    @pl.when(j == 0)
+                    def _():
+                        b = lax.rem(r, 2)
+                        pltpu.make_async_copy(a.at[0, pl.ds(0, TILE), pl.ds(0, kc)], res.at[b, :, pl.ds(0, kc)], l_res.at[b * KSTEPS + k]).wait()
+
                 def after(k):
+                    @pl.when(jnp.logical_and(r == 0, j == 0))
+                    def _():
+                        load_res(r + 1, k)
+
                     @pl.when(r + last < STRIPS)
                     def _():
                         load_stm(r + last, (j + 1) * (1 - last), k)
@@ -254,7 +274,7 @@
                         store_acc(r, j - 1).wait()
                         send(r, j - 1)
 
-                body_steps(res.at[lax.rem(r, 2)], acc.at[lax.rem(j, 2)], False, after)
+                body_steps(res.at[lax.rem(r, 2)], acc.at[lax.rem(j, 2)], False, before, after)
                 store_acc(r, j).start()
                 return carry
 
@@ -262,14 +282,14 @@
             store_acc(r, n - 1).wait()
             send(r, n - 1)
 
-            @pl.when(r >= 2)
-            def _():
-                finish(r - 2)
+            @pl.when(r >= LAG)
+            def _():
+                finish(r - LAG)
 
             return carry
 
         lax.fori_loop(0, STRIPS, strip, 0)
-        lax.fori_loop(STRIPS - 2, STRIPS, lambda r, carry: (finish(r), carry)[1], 0)
+        lax.fori_loop(STRIPS - LAG, STRIPS, lambda r, carry: (finish(r), carry)[1], 0)
         d2d.wait_send()
         lax.fori_loop(0, n_chunk, x_wait_send, 0)
 
@@ -281,18 +301,6 @@
             remote(a.at[layer], blk.at[layer], s_d.at[layer], r_d.at[layer], y, mate).start()
         lax.fori_loop(0, n_chunk, x_start, 0)
 
-        fc[0] = jnp.zeros((TILE, TILE), F32)
-
-        def zero(t, carry):
-            copies = [pltpu.make_async_copy(fc.at[0], out.at[2, lax.div(t, 4), at(lax.rem(t, 4) * TILE, TILE), pl.ds(q * TILE, TILE)], l_fa.at[q])
-                      for q in range(4)]
-            for copy in copies:
-                copy.start()
-            for copy in copies:
-                copy.wait()
-            return carry
-
-        lax.fori_loop(0, layers * n_strip, zero, 0)
         remote(a.at[lc], blk.at[0], s_d.at[0], r_d.at[0], y, mate).wait_recv()
 
         def region(ref, rows_first, c):
@@ -368,11 +376,14 @@
             return remote(region(awy.at[1], not is_left, c), region(out.at[y, 1 - lc], not is_left, c),
                           s_r.at[c], r_r.at[c], y, partner)
 
+        def away_late():
+            return remote(pieces[0], late, s_r.at[INSIDE], r_r.at[INSIDE], y, partner)
+
         def gather(c, owner):
             here = region(out.at[owner, 1 - lc], not is_left, c)
             return remote(here, here, s_y.at[3 * n_chunk + c], r_y.at[3 * n_chunk + c], 1 - y, g)
 
-        def add(c, local, received):
+        def add(c, local, received, store=None):
             def view(ref, q):
                 return ref.at[0, pl.ds(q * CHUNK, CHUNK), :] if is_left else ref.at[0, :, pl.ds(q * CHUNK, CHUNK)]
 
@@ -386,14 +397,40 @@
                 for copy in pairs[q]:
                     copy.wait()
                 view(fa, q)[...] = view(fa, q)[...] + view(fb, q)[...]
-                stores[q].start()
+                if store is None:
+                    stores[q].start()
+                else:
+                    store(q, view(fa, q), stores[q])
             for q in range(4):
                 stores[q].wait()
 
         def finish_away(c):
             spread(c).wait_recv()
-            add(c, awy.at[1], prv.at[2, 0])
-            away(c).start()
+
+            def store(q, total, inside):
+                @pl.when(c < INSIDE)
+                def _():
+                    inside.start()
+
+                for (first, stop), piece_ref in zip(PIECES, pieces):
+                    @pl.when(jnp.logical_and(c >= first, c < stop))
+                    def _(first=first, piece_ref=piece_ref):
+                        if is_left:
+                            pltpu.make_async_copy(total, piece_ref.at[c - first, :, pl.ds(q * TILE, TILE)], l_st.at[q]).start()
+                        else:
+                            for u in range(TILE // CHUNK):
+                                pltpu.make_async_copy(total.at[pl.ds(u * CHUNK, CHUNK), :],
+                                                      piece_ref.at[c - first, :, pl.ds(q * TILE + u * CHUNK, CHUNK)], l_st.at[q]).start()
+
+            add(c, awy.at[1], prv.at[2, 0], store)
+
+            @pl.when(c < INSIDE)
+            def _():
+                away(c).start()
+
+            @pl.when(c == INSIDE)
+            def _():
+                away_late().start()
 
         def finish_home(c):
             for b in range(2):
@@ -448,7 +485,11 @@
                         def _():
                             send_half(0 * t)
 
-                body_steps(res.at[lax.rem(c, 2), pl.ds(0, 2 * CHUNK), :], acc_view(t), not is_left, after)
+                        @pl.when(jnp.logical_and(c == n_chunk - 1, lax.rem(t, 2) == 1))
+                        def _():
+                            forward(lax.div(t, 2))
+
+                body_steps(res.at[lax.rem(c, 2), pl.ds(0, 2 * CHUNK), :], acc_view(t), not is_left, lambda k: None, after)
                 store_acc(c, t)(lambda copy: copy.start())
                 return carry
 
@@ -466,25 +507,26 @@
 
             return carry
 
-        def forwards(first, stop):
-            lax.fori_loop(first, stop, lambda c, carry: (forward(c), carry)[1], 0)
-
         lax.fori_loop(0, n_chunk, chunk, 0)
-        end = n_chunk - 1
-        forwards(0, n_chunk // 4)
-        finish_away(end)
-        forwards(n_chunk // 4, 5 * n_chunk // 8)
-        finish_home(end)
-        forwards(5 * n_chunk // 8, n_chunk)
+        for c in range(4, INSIDE):
+            forward(c)
+        finish_away(n_chunk - 1)
+        finish_home(n_chunk - 1)
 
         def drain(c, carry):
-            spread(c).wait_send()
             away(c).wait_send()
             gather(c, y).wait_send()
             gather(c, 1 - y).wait_recv()
             return carry
 
-        lax.fori_loop(0, n_chunk, drain, 0)
+        def drain_spread(c, carry):
+            spread(c).wait_send()
+            return carry
+
+        lax.fori_loop(0, INSIDE, drain, 0)
+        lax.fori_loop(0, n_chunk, drain_spread, 0)
+        away_late().wait_send()
+        away_late().wait_recv()
         for layer in range(layers):
             remote(a.at[layer], blk.at[layer], s_d.at[layer], r_d.at[layer], y, mate).wait_send()
         lax.fori_loop(0, n_chunk, x_wait_send, 0)
@@ -492,6 +534,122 @@
     pl.when(lax.rem(g, 3) == 0)(diagonal)
     pl.when(g == 1)(lambda: cross(True))
     pl.when(g == 2)(lambda: cross(False))
+
+
+def assembly(step, first, *refs):
+    n_in = len(first) + (step <= 2)
+    ins, (out, *scratch) = refs[:n_in], refs[n_in:]
+    buf, wide, l_in, l_out, l_win, l_wout = scratch
+    y = lax.axis_index("kk")
+    g = lax.axis_index("g")
+    depth = buf.shape[0]
+    lead = depth // 2
+
+    def at(start, size):
+        return pl.ds(pl.multiple_of(start, size), size)
+
+    def copies(n, where):
+        src = ins[-1]
+
+        def view(ref, t):
+            slot, layer, i, j = where(t)
+            return ref.at[slot, layer, at(i * TILE, TILE), at(j * TILE, TILE)]
+
+        def load(t):
+            b = lax.rem(t, depth)
+            return pltpu.make_async_copy(view(src, t), buf.at[b], l_in.at[b])
+
+        def store(t):
+            b = lax.rem(t, depth)
+            return pltpu.make_async_copy(buf.at[b], view(out, t), l_out.at[b])
+
+        def one(t, carry):
+            @pl.when(jnp.logical_and(t >= depth, t < n))
+            def _():
+                store(t - depth).wait()
+
+            @pl.when(t < n)
+            def _():
+                load(t).start()
+
+            @pl.when(t >= lead)
+            def _():
+                load(t - lead).wait()
+                store(t - lead).start()
+
+            return carry
+
+        lax.fori_loop(0, n + lead, one, 0)
+
+        def last(t, carry):
+            store(t).wait()
+            return carry
+
+        lax.fori_loop(max(n - depth, 0), n, last, 0)
+
+    def zeros():
+        buf[0] = jnp.zeros((TILE, TILE), F32)
+
+        def store(b, layer, t):
+            return pltpu.make_async_copy(buf.at[0], out.at[2, layer, at(lax.div(t, 4) * TILE, TILE), at(lax.rem(t, 4) * TILE, TILE)], l_out.at[b])
+
+        for layer in range(2):
+            for t in range(16):
+                store(t, layer, t).start()
+            for t in range(16):
+                store(t, layer, t).wait()
+
+    def away_results(is_left):
+        layer = 1 if is_left else 0
+        todo = [(k, c, n, (y if ours else 1 - y)) for k, (lo, hi, ours) in enumerate(first) for n, c in enumerate(range(lo, hi))]
+
+        def load(t):
+            k, _, n, _ = todo[t]
+            return pltpu.make_async_copy(ins[k].at[n], wide.at[t], l_win.at[t])
+
+        def whole(t):
+            _, c, _, slot = todo[t]
+            return pltpu.make_async_copy(wide.at[t], out.at[slot, layer, pl.ds(c * CHUNK, CHUNK), :], l_wout.at[t])
+
+        for t in range(len(todo)):
+            load(t).start()
+        for t in range(len(todo)):
+            _, c, _, slot = todo[t]
+            load(t).wait()
+            if not is_left:
+                whole(t).start()
+            else:
+                for u in range(out.shape[2] // CHUNK):
+                    pltpu.make_async_copy(wide.at[t, :, pl.ds(u * CHUNK, CHUNK)],
+                                          out.at[slot, layer, pl.ds(u * CHUNK, CHUNK), pl.ds(c * CHUNK, CHUNK)], l_wout.at[t]).start()
+        for t in range(len(todo)):
+            whole(t).wait()
+
+    def on_cross(is_left):
+        lc = 0 if is_left else 1
+        away_results(is_left)
+        if step == 0:
+            if is_left:
+                copies(16, lambda t: (lax.div(t, 8), 1 - lc, lax.rem(lax.div(t, 2), 4), lax.rem(t, 2)))
+            else:
+                copies(16, lambda t: (lax.div(t, 8), 1 - lc, lax.rem(lax.div(t, 4), 2), lax.rem(t, 4)))
+        elif step <= 2:
+            copies(16, lambda t: (step - 1, lc, lax.div(t, 4), lax.rem(t, 4)))
+        elif step == 3:
+            zeros()
+
+    @pl.when(g == 1)
+    def _():
+        on_cross(True)
+
+    @pl.when(g == 2)
+    def _():
+        on_cross(False)
+
+    if step < 3:
+        @pl.when(lax.rem(g, 3) == 0)
+        def _():
+            copies(32, lambda t: (step, lax.div(t, 16), lax.div(lax.rem(t, 16), 4), lax.rem(t, 4)))
 
 
 def solution(mesh):
@@ -502,16 +660,23 @@
         layers, rows, cols = a_loc.shape
         n_chunk = rows // CHUNK
         any_space = pl.BlockSpec(memory_space=pl.ANY)
-        result = pl.pallas_call(
+        slots_shape = jax.ShapeDtypeStruct((3, layers, rows, rows), F32)
+
+        def chunks_shape(n):
+            return jax.ShapeDtypeStruct((n, CHUNK, rows), F32)
+
+        slots, _, _, _, late, *pieces = pl.pallas_call(
             kernel,
             out_shape=(
-                jax.ShapeDtypeStruct((3, layers, rows, rows), F32),
+                slots_shape,
                 jax.ShapeDtypeStruct((3, rows, cols), a_loc.dtype),
-                jax.ShapeDtypeStruct((3, layers, rows, rows), F32),
+                slots_shape,
                 jax.ShapeDtypeStruct((2, rows, rows), F32),
+                chunks_shape(1),
+                *(chunks_shape(stop - start) for start, stop in PIECES),
             ),
             in_specs=[any_space],
-            out_specs=(any_space,) * 4,
+            out_specs=(any_space,) * (5 + len(PIECES)),
             scratch_shapes=[
                 pltpu.VMEM((2, TILE, cols), a_loc.dtype),
                 pltpu.VMEM((KSTEPS, TILE, cols // KSTEPS), a_loc.dtype),
@@ -521,13 +686,56 @@
                 pltpu.VMEM((2, TILE, TILE), F32),
                 dma((n_chunk,)), dma((2, n_chunk)), dma((2,)), dma((2,)),
                 dma((4 * n_chunk,)), dma((4 * STRIPS,)), dma((n_chunk,)), dma((n_chunk,)),
-                dma((2,)), dma((KSTEPS,)), dma((4,)), dma((4,)), dma((4,)), dma((4,)), dma((2,)),
+                dma((2 * KSTEPS,)), dma((KSTEPS,)), dma((4,)), dma((4,)), dma((4,)), dma((4,)), dma((2,)),
             ],
             compiler_params=pltpu.CompilerParams(
                 collective_id=0, has_side_effects=True, vmem_limit_bytes=63 * 2**20),
             cost_estimate=pl.CostEstimate(flops=10**12, bytes_accessed=10**9, transcendentals=0),
         )(a_loc)
-        return result[0][None]
+
+        other_chip = [(1, 2), (2, 1)]
+        other_half = [(1, 5), (5, 1), (2, 6), (6, 2)]
+
+        mine = [late] + [lax.ppermute(pieces[k], "g", other_chip) for k in range(1, len(PIECES))]
+        theirs = [lax.ppermute(mine[k], ("kk", "g"), other_half) for k in range(len(PIECES))]
+
+        def assemble(step, result, parts):
+            first = tuple(PIECES[k] + (ours,) for k, ours in parts)
+            arrays = [mine[k] if ours else theirs[k] for k, ours in parts]
+            n_wide = max(1, sum(stop - start for start, stop, _ in first))
+            sources = arrays + ([slots] if step <= 2 else [])
+            aliases = {}
+            operands = sources
+            if step > 0:
+                operands = [result] + sources
+                aliases = {0: 0}
+
+            def body(*refs):
+                assembly(step, first, *refs[len(operands) - len(sources):])
+
+            return pl.pallas_call(
+                body,
+                out_shape=slots_shape,
+                in_specs=[any_space] * len(operands),
+                out_specs=any_space,
+                input_output_aliases=aliases,
+                scratch_shapes=[
+                    pltpu.VMEM((16, TILE, TILE), F32), pltpu.VMEM((n_wide, CHUNK, rows), F32),
+                    dma((16,)), dma((16,)), dma((n_wide,)), dma((n_wide,)),
+                ],
+                compiler_params=pltpu.CompilerParams(vmem_limit_bytes=67043328),
+                cost_estimate=pl.CostEstimate(flops=10**10, bytes_accessed=10**8, transcendentals=0),
+            )(*operands)
+
+        result = assemble(0, None, [])
+        result = assemble(1, result, [(1, True)])
+        result = assemble(2, result, [(2, True), (0, True), (0, False)])
+        result = assemble(3, result, [(3, True), (1, False)])
+        result = assemble(4, result, [(4, True), (2, False)])
+        result = assemble(5, result, [(5, True), (3, False)])
+        result = assemble(6, result, [(6, True), (4, False)])
+        result = assemble(7, result, [(5, False), (6, False)])
+        return result[None]
 
     return jax.shard_map(local_part, mesh=mesh, in_specs=(P(None, ("m", "g"), "kk"),),
                          out_specs=P(("m", "g"), None, None, None, None), check_vma=False)

time: 1590 us -> 1560 us (0.981)
  the two profiles are of different devices: /device:TPU:2 before, /device:TPU:1 now
where the time goes in v2:
time: 1560 us
  Pallas kernels  1440 us (92%)
  waiting for transfers between devices  76.8 us (5%)
  starting transfers between devices  39.1 us (3%)
    pallas_call x1, Pallas kernels, local_part(): pl.pallas_call(kernel, out_shape=(slots_shape, jax.ShapeDtypeStruct((3, r...  1370 us
    pallas_call x8, Pallas kernels, assemble(): pl.pallas_call(body, out_shape=slots_shape, in_specs=[any_space] * len(op...  71.3 us
    ppermute x6, waiting for transfers between devices, local_part(): lax.ppermute(pieces[k], 'g', other_chip)  39.3 us
    ppermute x7, waiting for transfers between devices, local_part(): lax.ppermute(mine[k], ('kk', 'g'), other_half)  37.4 us
  transfers between devices with their start and end apart: 13, of which 5 were waited for; matrix products, arithmetic and copies ran while one was open for 0% of the time, Pallas kernels for 4%

profile of v2, /device:TPU:1, one launch (start us, length us, event | category | flops | bytes accessed | tf_op | source)
XLA Modules:
  0.0 1556.2 jit_solution(8855236693957987614)
XLA Ops:
  0.0 1368.7 %shard_map.17 = (f32[3,2,2048,2048]{3,2,1,0:T(8,128)}, bf16[3,2048,14336]{2,1,0:T(8,128)(2,1)}, f32[3,2,2048,2048]{3,2,1,0:T(8,128)}, f32[2,2048,2048]{2,1,0:T(8...) custom-call(bf16[2,2048,14336]{2,1,0:T(8,128)(2,1)} %a.1), custom_call_target="tpu_custom_call" | custom-call | flops 999999995904 | bytes 1000000000 | tf_op jit(solution)/shard_map/pallas_call | solution.py:668
  1368.7 4.5 collective-permute-start.1
  1373.2 1.9 collective-permute-start
  1375.2 3.6 collective-permute-start.9
  1378.8 1.9 collective-permute-start.3
  1380.7 3.1 collective-permute-start.2
  1383.8 24.6 %collective-permute-done.refs_1_ = f32[1,128,2048]{2,1,0:T(8,128)} collective-permute-done((f32[1,128,2048]{2,1,0:T(8,128)}, f32[1,128,2048]{2,1,0:T(8,128)}, u32[]{:S(2)}, u32[]{:S(2)}) %collective-permute-start) | collective-permute-done | bytes 1048608 | tf_op jit(solution)/shard_map/ppermute | solution.py:699
  1408.5 3.6 collective-permute-start.5
  1412.1 7.6 collective-permute-done.9.refs_1_
  1419.7 3.6 collective-permute-start.7
  1423.4 12.5 shard_map.18.refs_0_
  1435.9 0.0 collective-permute-done.2.refs_3_
  1435.9 3.1 collective-permute-start.4
  1439.0 0.0 collective-permute-done.1.refs_1_
  1439.0 2.2 collective-permute-start.6
  1441.2 14.7 shard_map.19.refs_0_
  1455.9 0.0 collective-permute-done.3.refs_1_
  1455.9 3.1 collective-permute-start.8
  1459.0 15.7 %shard_map.20.refs_0_ = f32[3,2,2048,2048]{3,2,1,0:T(8,128)} custom-call(f32[3,2,2048,2048]{3,2,1,0:T(8,128)} %shard_map.19.refs_0_, f32[2,128,2048]{2,1,0:T(8,128)} %collective-permute-done.1.refs_1_, f32[1,128,2048]{2,1,0:T(8,128)} %get-tuple-element.16.refs_2_, f32[1,128,2048]{2,1,0:T(8,128)} %collective-permute-done.2.refs_3_, ...), custom_call_target="tpu_custom_call", output_to_operand_aliasing={{}: (0, {})} | custom-call | flops 10000000000 | bytes 100000000 | tf_op jit(solution)/shard_map/pallas_call | solution.py:716
  1474.7 0.0 collective-permute-done.4.refs_2_
  1474.7 2.2 collective-permute-start.12
  1476.9 0.0 collective-permute-done.5.refs_1_
  1477.0 3.1 collective-permute-start.10
  1480.1 7.1 collective-permute-done.7.refs_1_
  1487.1 3.1 collective-permute-start.11
  1490.2 14.9 shard_map.21.refs_0_
  1505.1 0.0 collective-permute-done.6.refs_2_
  1505.1 3.5 shard_map.22.refs_0_
  1508.7 0.0 collective-permute-done.8.refs_2_
  1508.7 3.5 shard_map.23.refs_0_
  1512.3 18.1 %collective-permute-done.10.refs_2_ = f32[2,128,2048]{2,1,0:T(8,128)} collective-permute-done((f32[2,128,2048]{2,1,0:T(8,128)}, f32[2,128,2048]{2,1,0:T(8,128)}, u32[]{:S(2)}, u32[]{:S(2)}) %collective-permute-start.10) | collective-permute-done | bytes 2097184 | tf_op jit(solution)/shard_map/ppermute | solution.py:700
  1530.4 3.2 shard_map.24.refs_0_
  1533.6 0.0 collective-permute-done.12.refs_2_
  1533.6 19.3 %collective-permute-done.11.refs_1_ = f32[2,128,2048]{2,1,0:T(8,128)} collective-permute-done((f32[2,128,2048]{2,1,0:T(8,128)}, f32[2,128,2048]{2,1,0:T(8,128)}, u32[]{:S(2)}, u32[]{:S(2)}) %collective-permute-start.11) | collective-permute-done | bytes 2097184 | tf_op jit(solution)/shard_map/ppermute | solution.py:700
  1552.9 3.2 shard_map.25
Async XLA Ops:
  1368.7 70.3 %collective-permute-start.1 = (f32[2,128,2048]{2,1,0:T(8,128)}, f32[2,128,2048]{2,1,0:T(8,128)}, u32[]{:S(2)}, u32[]{:S(2)}) collective-permute-start(f32[2,128,2048]{2,1,0:T(8,128)} %get-tuple-element.15), channel_id=1, source_target_pairs={{1,2},{2,1},{5,6},{6,5}} | collective-permute-start | bytes 6291464 | tf_op jit(solution)/shard_map/ppermute | solution.py:699
  1373.2 35.3 %collective-permute-start = (f32[1,128,2048]{2,1,0:T(8,128)}, f32[1,128,2048]{2,1,0:T(8,128)}, u32[]{:S(2)}, u32[]{:S(2)}) collective-permute-start(f32[1,128,2048]{2,1,0:T(8,128)} %get-tuple-element.14), channel_id=1, source_target_pairs={{1,2},{2,1},{5,6},{6,5}} | collective-permute-start | bytes 3145736 | tf_op jit(solution)/shard_map/ppermute | solution.py:699
  1375.2 44.6 %collective-permute-start.9 = (f32[1,128,2048]{2,1,0:T(8,128)}, f32[1,128,2048]{2,1,0:T(8,128)}, u32[]{:S(2)}, u32[]{:S(2)}) collective-permute-start(f32[1,128,2048]{2,1,0:T(8,128)} %get-tuple-element.20), channel_id=1, source_target_pairs={{1,2},{2,1},{5,6},{6,5}} | collective-permute-start | bytes 3145736 | tf_op jit(solution)/shard_map/ppermute | solution.py:699
  1378.8 77.1 %collective-permute-start.3 = (f32[2,128,2048]{2,1,0:T(8,128)}, f32[2,128,2048]{2,1,0:T(8,128)}, u32[]{:S(2)}, u32[]{:S(2)}) collective-permute-start(f32[2,128,2048]{2,1,0:T(8,128)} %get-tuple-element.17), channel_id=1, source_target_pairs={{1,2},{2,1},{5,6},{6,5}} | collective-permute-start | bytes 6291464 | tf_op jit(solution)/shard_map/ppermute | solution.py:699
  1380.7 55.1 %collective-permute-start.2 = (f32[1,128,2048]{2,1,0:T(8,128)}, f32[1,128,2048]{2,1,0:T(8,128)}, u32[]{:S(2)}, u32[]{:S(2)}) collective-permute-start(f32[1,128,2048]{2,1,0:T(8,128)} %get-tuple-element.16.refs_2_), channel_id=1, source_target_pairs={{1,5},{5,1},{2,6},{6,2}} | collective-permute-start | bytes 3145736 | tf_op jit(solution)/shard_map/ppermute | solution.py:700
  1408.5 68.5 %collective-permute-start.5 = (f32[2,128,2048]{2,1,0:T(8,128)}, f32[2,128,2048]{2,1,0:T(8,128)}, u32[]{:S(2)}, u32[]{:S(2)}) collective-permute-start(f32[2,128,2048]{2,1,0:T(8,128)} %get-tuple-element.18), channel_id=1, source_target_pairs={{1,2},{2,1},{5,6},{6,5}} | collective-permute-start | bytes 6291464 | tf_op jit(solution)/shard_map/ppermute | solution.py:699
  1419.7 67.4 %collective-permute-start.7 = (f32[2,128,2048]{2,1,0:T(8,128)}, f32[2,128,2048]{2,1,0:T(8,128)}, u32[]{:S(2)}, u32[]{:S(2)}) collective-permute-start(f32[2,128,2048]{2,1,0:T(8,128)} %get-tuple-element.19), channel_id=1, source_target_pairs={{1,2},{2,1},{5,6},{6,5}} | collective-permute-start | bytes 6291464 | tf_op jit(solution)/shard_map/ppermute | solution.py:699
  1435.9 38.8 %collective-permute-start.4 = (f32[1,128,2048]{2,1,0:T(8,128)}, f32[1,128,2048]{2,1,0:T(8,128)}, u32[]{:S(2)}, u32[]{:S(2)}) collective-permute-start(f32[1,128,2048]{2,1,0:T(8,128)} %collective-permute-done.refs_1_), channel_id=1, source_target_pairs={{1,5},{5,1},{2,6},{6,2}} | collective-permute-start | bytes 3145736 | tf_op jit(solution)/shard_map/ppermute | solution.py:700
  1439.0 66.1 %collective-permute-start.6 = (f32[2,128,2048]{2,1,0:T(8,128)}, f32[2,128,2048]{2,1,0:T(8,128)}, u32[]{:S(2)}, u32[]{:S(2)}) collective-permute-start(f32[2,128,2048]{2,1,0:T(8,128)} %collective-permute-done.1.refs_1_), channel_id=1, source_target_pairs={{1,5},{5,1},{2,6},{6,2}} | collective-permute-start | bytes 6291464 | tf_op jit(solution)/shard_map/ppermute | solution.py:700
  1455.9 52.8 %collective-permute-start.8 = (f32[2,128,2048]{2,1,0:T(8,128)}, f32[2,128,2048]{2,1,0:T(8,128)}, u32[]{:S(2)}, u32[]{:S(2)}) collective-permute-start(f32[2,128,2048]{2,1,0:T(8,128)} %collective-permute-done.3.refs_1_), channel_id=1, source_target_pairs={{1,5},{5,1},{2,6},{6,2}} | collective-permute-start | bytes 6291464 | tf_op jit(solution)/shard_map/ppermute | solution.py:700
  1474.7 58.8 %collective-permute-start.12 = (f32[1,128,2048]{2,1,0:T(8,128)}, f32[1,128,2048]{2,1,0:T(8,128)}, u32[]{:S(2)}, u32[]{:S(2)}) collective-permute-start(f32[1,128,2048]{2,1,0:T(8,128)} %collective-permute-done.9.refs_1_), channel_id=1, source_target_pairs={{1,5},{5,1},{2,6},{6,2}} | collective-permute-start | bytes 3145736 | tf_op jit(solution)/shard_map/ppermute | solution.py:700
  1477.0 53.4 %collective-permute-start.10 = (f32[2,128,2048]{2,1,0:T(8,128)}, f32[2,128,2048]{2,1,0:T(8,128)}, u32[]{:S(2)}, u32[]{:S(2)}) collective-permute-start(f32[2,128,2048]{2,1,0:T(8,128)} %collective-permute-done.5.refs_1_), channel_id=1, source_target_pairs={{1,5},{5,1},{2,6},{6,2}} | collective-permute-start | bytes 6291464 | tf_op jit(solution)/shard_map/ppermute | solution.py:700
  1487.1 65.7 %collective-permute-start.11 = (f32[2,128,2048]{2,1,0:T(8,128)}, f32[2,128,2048]{2,1,0:T(8,128)}, u32[]{:S(2)}, u32[]{:S(2)}) collective-permute-start(f32[2,128,2048]{2,1,0:T(8,128)} %collective-permute-done.7.refs_1_), channel_id=1, source_target_pairs={{1,5},{5,1},{2,6},{6,2}} | collective-permute-start | bytes 6291464 | tf_op jit(solution)/shard_map/ppermute | solution.py:700

commit v3 on v2

--- a/solution.py
+++ b/solution.py
@@ -15,18 +15,20 @@
 STRIPS = 24
 KSTEPS = 2
 LAG = 4
-INSIDE = 5
-PIECES = ((5, 6), (6, 7), (7, 9), (9, 11), (11, 13), (13, 15), (15, 16))
-
-
-def kernel(a, out, blk, prv, awy, late, *refs):
-    pieces, refs = refs[:len(PIECES)], refs[len(PIECES):]
-    work(a, out, blk, prv, awy, late, pieces, *refs)
-
-
-def work(a, out, blk, prv, awy, late, pieces, res, stm, acc, fa, fb, fc,
-           s_x, r_x, s_d, r_d, s_y, r_y, s_r, r_r,
-           l_res, l_stm, l_acc, l_fa, l_fb, l_st, l_tr):
+PACKED = 264
+WHOLE = 2
+INSIDE = 4
+PIECES = ((4, 8), (8, 11), (11, 14), (14, 16))
+
+
+def kernel(a, out, blk, prv, awy, pkl, pkr, late, *refs):
+    both, pieces, refs = refs[:WHOLE], refs[WHOLE:WHOLE + len(PIECES)], refs[WHOLE + len(PIECES):]
+    work(a, out, blk, prv, awy, pkl, pkr, late, both, pieces, *refs)
+
+
+def work(a, out, blk, prv, awy, pkl, pkr, late, both, pieces, res, stm, acc, fa, fb, fc, pk, fpa, fpb,
+         s_x, r_x, s_d, r_d, s_y, r_y, s_r, r_r,
+         l_res, l_stm, l_acc, l_fa, l_fb, l_st, l_tr, l_pk):
     m = lax.axis_index("m")
     y = lax.axis_index("kk")
     g = lax.axis_index("g")
@@ -42,12 +44,13 @@
     def remote(src, dst, ss, rs, kk2, g2):
         return pltpu.make_async_remote_copy(src, dst, ss, rs, device_id=(m, kk2, g2), device_id_type=MESH)
 
-    barrier = pltpu.get_barrier_semaphore()
-    me = y * 4 + g
-    for step in range(1, 8):
-        other = lax.rem(me + step, 8)
-        pl.semaphore_signal(barrier, inc=1, device_id=(m, lax.div(other, 4), lax.rem(other, 4)), device_id_type=MESH)
-    pl.semaphore_wait(barrier, 7)
+    def enter():
+        barrier = pltpu.get_barrier_semaphore()
+        me = y * 4 + g
+        for step in range(1, 8):
+            other = lax.rem(me + step, 8)
+            pl.semaphore_signal(barrier, inc=1, device_id=(m, lax.div(other, 4), lax.rem(other, 4)), device_id_type=MESH)
+        pl.semaphore_wait(barrier, 7)
 
     def x_in(c):
         part = lax.rem(g, 2)
@@ -137,11 +140,47 @@
 
             return remote(part(out), part(prv), s_y.at[lax.rem(r, 8) * 4 + j], r_y.at[r * 4 + j], 1 - y, g)
 
+        def packed(r):
+            e = lax.rem(r, 8) + 8 * lax.div(phase(r)[0], 2)
+            return remote(pkl.at[e], pkr.at[e], s_y.at[32 + lax.rem(r, 8)], r_y.at[4 * STRIPS + e], 1 - y, g)
+
+        def store_packed(r):
+            return pltpu.make_async_copy(pk, pkl.at[lax.rem(r, 8) + 8 * lax.div(phase(r)[0], 2)], l_pk.at[0])
+
+        def load_packed(r):
+            e = lax.rem(r, 8) + 8 * lax.div(phase(r)[0], 2)
+            return pltpu.make_async_copy(pkl.at[e], fpa, l_pk.at[1]), pltpu.make_async_copy(pkr.at[e], fpb, l_pk.at[2])
+
+        row_id = lax.broadcasted_iota(jnp.int32, (128, 128), 0)
+        col_id = lax.broadcasted_iota(jnp.int32, (128, 128), 1)
+
+        def pack(tile):
+            ends = []
+            for h in range(2):
+                one, two = 256 * h, 256 * h + 128
+                first = tile[pl.ds(one, 128), pl.ds(one, 128)]
+                second = tile[pl.ds(two, 128), pl.ds(two, 128)]
+                pk[pl.ds(128 * h, 128), :] = jnp.where(row_id > col_id, first, second.T)
+                ends.append(jnp.sum(jnp.where(row_id == col_id, first, 0.0), axis=0, keepdims=True))
+            pk[pl.ds(256, 8), :] = jnp.where(row_id[:8] == 0, ends[0], ends[1])
+
+        def unpack(tile):
+            fpa[...] = fpa[...] + fpb[...]
+            for h in range(2):
+                one, two = 256 * h, 256 * h + 128
+                both = fpa[pl.ds(128 * h, 128), :]
+                turned = both.T
+                ends = fpa[pl.ds(256 + h, 1), :]
+                tile[pl.ds(one, 128), pl.ds(one, 128)] = jnp.where(row_id > col_id, both, jnp.where(row_id == col_id, ends, turned))
+                tile[pl.ds(two, 128), pl.ds(two, 128)] = jnp.where(row_id <= col_id, both, turned)
+
         def send(r, j):
             @pl.when(is_diag(r, j))
             def _():
-                for q in range(4):
-                    lower(r, j, q * 128, 128, (q + 1) * 128).start()
+                for q in range(1, 4):
+                    lower(r, j, q * 128, 128, q * 128).start()
+                store_packed(r).wait()
+                packed(r).start()
 
             @pl.when(jnp.logical_not(is_diag(r, j)))
             def _():
@@ -150,9 +189,11 @@
         def wait_exchange(r, j):
             @pl.when(is_diag(r, j))
             def _():
-                sized = lower(r, j, 0, 320, TILE)
+                sized = lower(r, j, 0, 192, TILE)
                 sized.wait_send()
                 sized.wait_recv()
+                packed(r).wait_send()
+                packed(r).wait_recv()
 
             @pl.when(jnp.logical_not(is_diag(r, j)))
             def _():
@@ -176,6 +217,11 @@
                 for copy in loads(j):
                     copy.start()
 
+                @pl.when(is_diag(r, j))
+                def _():
+                    for copy in load_packed(r):
+                        copy.start()
+
             def main_store(j):
                 return pltpu.make_async_copy(fa.at[lax.rem(j, 2)], tile_of(out, r, i, j), l_st.at[lax.rem(j, 2)])
 
@@ -217,6 +263,9 @@
                     at_row = lax.broadcasted_iota(jnp.int32, (TILE, TILE), 0)
                     at_col = lax.broadcasted_iota(jnp.int32, (TILE, TILE), 1)
                     fa[b] = jnp.where(at_row >= at_col, total, total.T)
+                    for copy in load_packed(r):
+                        copy.wait()
+                    unpack(fa.at[b])
 
                 main_store(j).start()
                 return carry
@@ -229,11 +278,14 @@
 
             wait_stores(n - 1)
 
-        for k in range(KSTEPS):
+        load_res(0, 0)
+        load_stm(0, 0, 0)
+        enter()
+        lax.fori_loop(0, n_chunk, x_start, 0)
+        for k in range(1, KSTEPS):
             load_res(0, k)
             load_stm(0, 0, k)
         d2d.start()
-        lax.fori_loop(0, n_chunk, x_start, 0)
 
         def strip(r, carry):
             @pl.when(r == 7)
@@ -269,13 +321,24 @@
                     def _():
                         load_stm(r + last, (j + 1) * (1 - last), k)
 
-                    @pl.when(jnp.logical_and(k == 0, j >= 1))
+                    @pl.when(jnp.logical_and(k == 0, jnp.logical_and(j >= 1, r + j >= 2)))
                     def _():
                         store_acc(r, j - 1).wait()
                         send(r, j - 1)
 
                 body_steps(res.at[lax.rem(r, 2)], acc.at[lax.rem(j, 2)], False, before, after)
                 store_acc(r, j).start()
+
+                @pl.when(is_diag(r, j))
+                def _():
+                    pack(acc.at[lax.rem(j, 2)])
+                    store_packed(r).start()
+
+                @pl.when(jnp.logical_and(r == 0, j == 0))
+                def _():
+                    store_acc(r, j).wait()
+                    send(r, j)
+
                 return carry
 
             lax.fori_loop(0, n, tile, 0)
@@ -297,9 +360,10 @@
         lc = 0 if is_left else 1
         mate = 0 if is_left else 3
         partner = 2 if is_left else 1
+        enter()
+        lax.fori_loop(0, n_chunk, x_start, 0)
         for layer in range(layers):
             remote(a.at[layer], blk.at[layer], s_d.at[layer], r_d.at[layer], y, mate).start()
-        lax.fori_loop(0, n_chunk, x_start, 0)
 
         remote(a.at[lc], blk.at[0], s_d.at[0], r_d.at[0], y, mate).wait_recv()
 
@@ -376,8 +440,11 @@
             return remote(region(awy.at[1], not is_left, c), region(out.at[y, 1 - lc], not is_left, c),
                           s_r.at[c], r_r.at[c], y, partner)
 
-        def away_late():
-            return remote(pieces[0], late, s_r.at[INSIDE], r_r.at[INSIDE], y, partner)
+        def away_late(c):
+            return remote(pieces[0].at[c - INSIDE], late.at[c - INSIDE], s_r.at[c], r_r.at[c], y, partner)
+
+        def gather_here(k):
+            return remote(both[k].at[0], both[k].at[1], s_y.at[3 * n_chunk + k], r_y.at[3 * n_chunk + k], 1 - y, g)
 
         def gather(c, owner):
             here = region(out.at[owner, 1 - lc], not is_left, c)
@@ -408,29 +475,42 @@
             spread(c).wait_recv()
 
             def store(q, total, inside):
-                @pl.when(c < INSIDE)
+                @pl.when(jnp.logical_and(c >= WHOLE, c < INSIDE))
                 def _():
                     inside.start()
+
+                def put(dst):
+                    if is_left:
+                        pltpu.make_async_copy(total, dst.at[:, pl.ds(q * TILE, TILE)], l_st.at[q]).start()
+                    else:
+                        for u in range(TILE // CHUNK):
+                            pltpu.make_async_copy(total.at[pl.ds(u * CHUNK, CHUNK), :],
+                                                  dst.at[:, pl.ds(q * TILE + u * CHUNK, CHUNK)], l_st.at[q]).start()
+
+                for k in range(WHOLE):
+                    @pl.when(c == k)
+                    def _(k=k):
+                        put(both[k].at[0])
 
                 for (first, stop), piece_ref in zip(PIECES, pieces):
                     @pl.when(jnp.logical_and(c >= first, c < stop))
                     def _(first=first, piece_ref=piece_ref):
-                        if is_left:
-                            pltpu.make_async_copy(total, piece_ref.at[c - first, :, pl.ds(q * TILE, TILE)], l_st.at[q]).start()
-                        else:
-                            for u in range(TILE // CHUNK):
-                                pltpu.make_async_copy(total.at[pl.ds(u * CHUNK, CHUNK), :],
-                                                      piece_ref.at[c - first, :, pl.ds(q * TILE + u * CHUNK, CHUNK)], l_st.at[q]).start()
+                        put(piece_ref.at[c - first])
 
             add(c, awy.at[1], prv.at[2, 0], store)
 
-            @pl.when(c < INSIDE)
+            for k in range(WHOLE):
+                @pl.when(c == k)
+                def _(k=k):
+                    gather_here(k).start()
+
+            @pl.when(jnp.logical_and(c >= WHOLE, c < INSIDE))
             def _():
                 away(c).start()
 
-            @pl.when(c == INSIDE)
-            def _():
-                away_late().start()
+            @pl.when(jnp.logical_and(c >= INSIDE, c < PIECES[0][1]))
+            def _():
+                away_late(c).start()
 
         def finish_home(c):
             for b in range(2):
@@ -485,9 +565,9 @@
                         def _():
                             send_half(0 * t)
 
-                        @pl.when(jnp.logical_and(c == n_chunk - 1, lax.rem(t, 2) == 1))
+                        @pl.when(jnp.logical_and(c == n_chunk - 1, jnp.logical_and(lax.rem(t, 3) == 2, t < 3 * (INSIDE - WHOLE))))
                         def _():
-                            forward(lax.div(t, 2))
+                            forward(WHOLE + lax.div(t, 3))
 
                 body_steps(res.at[lax.rem(c, 2), pl.ds(0, 2 * CHUNK), :], acc_view(t), not is_left, lambda k: None, after)
                 store_acc(c, t)(lambda copy: copy.start())
@@ -508,8 +588,6 @@
             return carry
 
         lax.fori_loop(0, n_chunk, chunk, 0)
-        for c in range(4, INSIDE):
-            forward(c)
         finish_away(n_chunk - 1)
         finish_home(n_chunk - 1)
 
@@ -523,10 +601,14 @@
             spread(c).wait_send()
             return carry
 
-        lax.fori_loop(0, INSIDE, drain, 0)
+        for k in range(WHOLE):
+            gather_here(k).wait_send()
+            gather_here(k).wait_recv()
+        lax.fori_loop(WHOLE, INSIDE, drain, 0)
         lax.fori_loop(0, n_chunk, drain_spread, 0)
-        away_late().wait_send()
-        away_late().wait_recv()
+        for c in range(*PIECES[0]):
+            away_late(c).wait_send()
+            away_late(c).wait_recv()
         for layer in range(layers):
             remote(a.at[layer], blk.at[layer], s_d.at[layer], r_d.at[layer], y, mate).wait_send()
         lax.fori_loop(0, n_chunk, x_wait_send, 0)
@@ -601,7 +683,10 @@
 
     def away_results(is_left):
         layer = 1 if is_left else 0
-        todo = [(k, c, n, (y if ours else 1 - y)) for k, (lo, hi, ours) in enumerate(first) for n, c in enumerate(range(lo, hi))]
+        todo = []
+        for k, ranges in enumerate(first):
+            chunks = [(c, slot) for span, slot in zip(ranges, (y, 1 - y)) if span for c in range(*span)]
+            todo += [(k, c, n, slot) for n, (c, slot) in enumerate(chunks)]
 
         def load(t):
             k, _, n, _ = todo[t]
@@ -614,7 +699,7 @@
         for t in range(len(todo)):
             load(t).start()
         for t in range(len(todo)):
-            _, c, _, slot = todo[t]
+            k, c, _, slot = todo[t]
             load(t).wait()
             if not is_left:
                 whole(t).start()
@@ -630,13 +715,13 @@
         away_results(is_left)
         if step == 0:
             if is_left:
-                copies(16, lambda t: (lax.div(t, 8), 1 - lc, lax.rem(lax.div(t, 2), 4), lax.rem(t, 2)))
+                copies(8, lambda t: (lax.div(t, 4), 1 - lc, lax.rem(t, 4), 0))
             else:
-                copies(16, lambda t: (lax.div(t, 8), 1 - lc, lax.rem(lax.div(t, 4), 2), lax.rem(t, 4)))
+                copies(8, lambda t: (lax.div(t, 4), 1 - lc, 0, lax.rem(t, 4)))
         elif step <= 2:
             copies(16, lambda t: (step - 1, lc, lax.div(t, 4), lax.rem(t, 4)))
-        elif step == 3:
-            zeros()
+            if step == 2:
+                zeros()
 
     @pl.when(g == 1)
     def _():
@@ -665,18 +750,21 @@
         def chunks_shape(n):
             return jax.ShapeDtypeStruct((n, CHUNK, rows), F32)
 
-        slots, _, _, _, late, *pieces = pl.pallas_call(
+        slots, _, _, _, _, _, late, *others = pl.pallas_call(
             kernel,
             out_shape=(
                 slots_shape,
                 jax.ShapeDtypeStruct((3, rows, cols), a_loc.dtype),
                 slots_shape,
                 jax.ShapeDtypeStruct((2, rows, rows), F32),
-                chunks_shape(1),
+                jax.ShapeDtypeStruct((16, PACKED, 128), F32),
+                jax.ShapeDtypeStruct((16, PACKED, 128), F32),
+                chunks_shape(PIECES[0][1] - PIECES[0][0]),
+                *(chunks_shape(2) for _ in range(WHOLE)),
                 *(chunks_shape(stop - start) for start, stop in PIECES),
             ),
             in_specs=[any_space],
-            out_specs=(any_space,) * (5 + len(PIECES)),
+            out_specs=(any_space,) * (7 + WHOLE + len(PIECES)),
             scratch_shapes=[
                 pltpu.VMEM((2, TILE, cols), a_loc.dtype),
                 pltpu.VMEM((KSTEPS, TILE, cols // KSTEPS), a_loc.dtype),
@@ -684,25 +772,32 @@
                 pltpu.VMEM((2, TILE, TILE), F32),
                 pltpu.VMEM((2, TILE, TILE), F32),
                 pltpu.VMEM((2, TILE, TILE), F32),
+                pltpu.VMEM((PACKED, 128), F32),
+                pltpu.VMEM((PACKED, 128), F32),
+                pltpu.VMEM((PACKED, 128), F32),
                 dma((n_chunk,)), dma((2, n_chunk)), dma((2,)), dma((2,)),
-                dma((4 * n_chunk,)), dma((4 * STRIPS,)), dma((n_chunk,)), dma((n_chunk,)),
-                dma((2 * KSTEPS,)), dma((KSTEPS,)), dma((4,)), dma((4,)), dma((4,)), dma((4,)), dma((2,)),
+                dma((4 * n_chunk,)), dma((4 * STRIPS + 16,)), dma((n_chunk,)), dma((n_chunk,)),
+                dma((2 * KSTEPS,)), dma((KSTEPS,)), dma((4,)), dma((4,)), dma((4,)), dma((4,)), dma((2,)), dma((3,)),
             ],
             compiler_params=pltpu.CompilerParams(
                 collective_id=0, has_side_effects=True, vmem_limit_bytes=63 * 2**20),
             cost_estimate=pl.CostEstimate(flops=10**12, bytes_accessed=10**9, transcendentals=0),
         )(a_loc)
 
+        both, pieces = others[:WHOLE], others[WHOLE:]
         other_chip = [(1, 2), (2, 1)]
         other_half = [(1, 5), (5, 1), (2, 6), (6, 2)]
 
-        mine = [late] + [lax.ppermute(pieces[k], "g", other_chip) for k in range(1, len(PIECES))]
-        theirs = [lax.ppermute(mine[k], ("kk", "g"), other_half) for k in range(len(PIECES))]
+        n_pieces = len(PIECES)
+        mine = [late] + [lax.ppermute(pieces[k], "g", other_chip) for k in range(1, n_pieces)]
+        theirs = [lax.ppermute(mine[k], ("kk", "g"), other_half) for k in range(n_pieces)]
+        pairs = [lax.ppermute(both[k], "g", other_chip) for k in range(WHOLE)]
 
         def assemble(step, result, parts):
-            first = tuple(PIECES[k] + (ours,) for k, ours in parts)
-            arrays = [mine[k] if ours else theirs[k] for k, ours in parts]
-            n_wide = max(1, sum(stop - start for start, stop, _ in first))
+            first = tuple(((k, k + 1),) * 2 if kind == "pair" else (PIECES[k], None) if kind == "mine" else (None, PIECES[k])
+                          for kind, k in parts)
+            arrays = [{"mine": mine, "theirs": theirs, "pair": pairs}[kind][k] for kind, k in parts]
+            n_wide = max(1, sum(stop - start for ranges in first for start, stop in filter(None, ranges)))
             sources = arrays + ([slots] if step <= 2 else [])
             aliases = {}
             operands = sources
@@ -728,13 +823,12 @@
             )(*operands)
 
         result = assemble(0, None, [])
-        result = assemble(1, result, [(1, True)])
-        result = assemble(2, result, [(2, True), (0, True), (0, False)])
-        result = assemble(3, result, [(3, True), (1, False)])
-        result = assemble(4, result, [(4, True), (2, False)])
-        result = assemble(5, result, [(5, True), (3, False)])
-        result = assemble(6, result, [(6, True), (4, False)])
-        result = assemble(7, result, [(5, False), (6, False)])
+        result = assemble(1, result, [("mine", 0)])
+        result = assemble(2, result, [("mine", 1)])
+        result = assemble(3, result, [("mine", 2), ("theirs", 0)])
+        result = assemble(4, result, [("mine", 3), ("theirs", 1)])
+        result = assemble(5, result, [("pair", 0), ("theirs", 2)])
+        result = assemble(6, result, [("pair", 1), ("theirs", 3)])
         return result[None]
 
     return jax.shard_map(local_part, mesh=mesh, in_specs=(P(None, ("m", "g"), "kk"),),

time: 1560 us -> 1500 us (0.962)
  Pallas kernels: 1440 us -> 1410 us
  waiting for transfers between devices: 76.8 us -> 56.9 us
    ppermute x7 -> x4, waiting for transfers between devices: 37.4 us -> 3 us  [local_part(): lax.ppermute(mine[k], ('kk', 'g'), other_half)]
    pallas_call x1, Pallas kernels: 1370 us -> 1340 us  [local_part(): pl.pallas_call(kernel, out_shape=(slots_shape, jax.ShapeDtypeStruct((3, r...]
    ppermute x6 -> x3, waiting for transfers between devices: 39.3 us -> 47.6 us  [local_part(): lax.ppermute(pieces[k], 'g', other_chip)]
    pallas_call x8 -> x7, Pallas kernels: 71.3 us -> 68.7 us  [assemble(): pl.pallas_call(body, out_shape=slots_shape, in_specs=[any_space] * len(op...]
  transfers between devices with their start and end apart: 13 -> 9, of which waited for: 5 -> 4; matrix products, arithmetic and copies ran while one was open for 0% -> 0% of each run, Pallas kernels for 4% -> 4%
where the time goes in v3:
time: 1500 us
  Pallas kernels  1410 us (94%)
  waiting for transfers between devices  56.9 us (4%)
  starting transfers between devices  27.8 us (2%)
    pallas_call x1, Pallas kernels, local_part(): pl.pallas_call(kernel, out_shape=(slots_shape, jax.ShapeDtypeStruct((3, r...  1340 us
    pallas_call x7, Pallas kernels, assemble(): pl.pallas_call(body, out_shape=slots_shape, in_specs=[any_space] * len(op...  68.7 us
    ppermute x3, waiting for transfers between devices, local_part(): lax.ppermute(pieces[k], 'g', other_chip)  47.6 us
  transfers between devices with their start and end apart: 9, of which 4 were waited for; matrix products, arithmetic and copies ran while one was open for 0% of the time, Pallas kernels for 4%

profile of v3, /device:TPU:1, one launch (start us, length us, event | category | flops | bytes accessed | tf_op | source)
XLA Modules:
  0.0 1496.7 jit_solution(104496119386739073)
XLA Ops:
  0.0 1343.2 %shard_map.17 = (f32[3,2,2048,2048]{3,2,1,0:T(8,128)}, bf16[3,2048,14336]{2,1,0:T(8,128)(2,1)}, f32[3,2,2048,2048]{3,2,1,0:T(8,128)}, f32[2,2048,2048]{2,1,0:T(8...) custom-call(bf16[2,2048,14336]{2,1,0:T(8,128)(2,1)} %a.1), custom_call_target="tpu_custom_call" | custom-call | flops 999999995904 | bytes 1000000000 | tf_op jit(solution)/shard_map/pallas_call | solution.py:753
  1343.2 3.9 collective-permute-start
  1347.1 1.9 collective-permute-start.1
  1349.1 3.6 collective-permute-start.2
  1352.6 3.5 collective-permute-start.3
  1356.1 2.1 collective-permute-start.5
  1358.2 24.2 %collective-permute-done.refs_1_ = f32[3,128,2048]{2,1,0:T(8,128)} collective-permute-done((f32[3,128,2048]{2,1,0:T(8,128)}, f32[3,128,2048]{2,1,0:T(8,128)}, u32[]{:S(2)}, u32[]{:S(2)}) %collective-permute-start) | collective-permute-done | bytes 3145760 | tf_op jit(solution)/shard_map/ppermute | solution.py:792
  1382.4 3.5 collective-permute-start.4
  1385.9 6.7 shard_map.18.refs_0_
  1392.6 23.4 %collective-permute-done.1.refs_1_ = f32[3,128,2048]{2,1,0:T(8,128)} collective-permute-done((f32[3,128,2048]{2,1,0:T(8,128)}, f32[3,128,2048]{2,1,0:T(8,128)}, u32[]{:S(2)}, u32[]{:S(2)}) %collective-permute-start.1) | collective-permute-done | bytes 3145760 | tf_op jit(solution)/shard_map/ppermute | solution.py:792
  1416.1 3.5 collective-permute-start.6
  1419.6 15.7 %shard_map.19.refs_0_ = f32[3,2,2048,2048]{3,2,1,0:T(8,128)} custom-call(f32[3,2,2048,2048]{3,2,1,0:T(8,128)} %shard_map.18.refs_0_, f32[4,128,2048]{2,1,0:T(8,128)} %get-tuple-element.13.refs_1_, f32[3,2,2048,2048]{3,2,1,0:T(8,128)} %get-tuple-element.12.refs_0_.refs_2_), custom_call_target="tpu_custom_call", output_to_operand_aliasing={{}: (0, {})} | custom-call | flops 10000000000 | bytes 100000000 | tf_op jit(solution)/shard_map/pallas_call | solution.py:811
  1435.4 27.1 %shard_map.20.refs_0_ = f32[3,2,2048,2048]{3,2,1,0:T(8,128)} custom-call(f32[3,2,2048,2048]{3,2,1,0:T(8,128)} %shard_map.19.refs_0_, f32[3,128,2048]{2,1,0:T(8,128)} %collective-permute-done.refs_1_, f32[3,2,2048,2048]{3,2,1,0:T(8,128)} %get-tuple-element.12.refs_0_.refs_2_), custom_call_target="tpu_custom_call", output_to_operand_aliasing={{}: (0, {})} | custom-call | flops 10000000000 | bytes 100000000 | tf_op jit(solution)/shard_map/pallas_call | solution.py:811
  1462.5 0.0 collective-permute-done.3.refs_1_
  1462.5 3.6 collective-permute-start.7
  1466.0 0.0 collective-permute-done.2.refs_2_
  1466.1 2.2 collective-permute-start.8
  1468.3 6.3 shard_map.21.refs_0_
  1474.6 0.0 collective-permute-done.4.refs_2_
  1474.6 4.6 shard_map.22.refs_0_
  1479.3 0.0 collective-permute-done.5.refs_1_
  1479.3 0.0 collective-permute-done.6.refs_2_
  1479.3 4.6 shard_map.23.refs_0_
  1483.9 6.2 collective-permute-done.7.refs_1_
  1490.2 3.0 collective-permute-done.8.refs_2_
  1493.1 3.5 shard_map.24
Async XLA Ops:
  1343.2 39.2 %collective-permute-start = (f32[3,128,2048]{2,1,0:T(8,128)}, f32[3,128,2048]{2,1,0:T(8,128)}, u32[]{:S(2)}, u32[]{:S(2)}) collective-permute-start(f32[3,128,2048]{2,1,0:T(8,128)} %get-tuple-element.14), channel_id=1, source_target_pairs={{1,2},{2,1},{5,6},{6,5}} | collective-permute-start | bytes 9437192 | tf_op jit(solution)/shard_map/ppermute | solution.py:792
  1347.1 69.0 %collective-permute-start.1 = (f32[3,128,2048]{2,1,0:T(8,128)}, f32[3,128,2048]{2,1,0:T(8,128)}, u32[]{:S(2)}, u32[]{:S(2)}) collective-permute-start(f32[3,128,2048]{2,1,0:T(8,128)} %get-tuple-element.15), channel_id=1, source_target_pairs={{1,2},{2,1},{5,6},{6,5}} | collective-permute-start | bytes 9437192 | tf_op jit(solution)/shard_map/ppermute | solution.py:792
  1349.1 117.0 %collective-permute-start.2 = (f32[4,128,2048]{2,1,0:T(8,128)}, f32[4,128,2048]{2,1,0:T(8,128)}, u32[]{:S(2)}, u32[]{:S(2)}) collective-permute-start(f32[4,128,2048]{2,1,0:T(8,128)} %get-tuple-element.13.refs_1_), channel_id=1, source_target_pairs={{1,5},{5,1},{2,6},{6,2}} | collective-permute-start | bytes 12582920 | tf_op jit(solution)/shard_map/ppermute | solution.py:793
  1352.6 109.9 %collective-permute-start.3 = (f32[2,128,2048]{2,1,0:T(8,128)}, f32[2,128,2048]{2,1,0:T(8,128)}, u32[]{:S(2)}, u32[]{:S(2)}) collective-permute-start(f32[2,128,2048]{2,1,0:T(8,128)} %get-tuple-element.16), channel_id=1, source_target_pairs={{1,2},{2,1},{5,6},{6,5}} | collective-permute-start | bytes 6291464 | tf_op jit(solution)/shard_map/ppermute | solution.py:792
  1356.1 123.2 %collective-permute-start.5 = (f32[2,128,2048]{2,1,0:T(8,128)}, f32[2,128,2048]{2,1,0:T(8,128)}, u32[]{:S(2)}, u32[]{:S(2)}) collective-permute-start(f32[2,128,2048]{2,1,0:T(8,128)} %get-tuple-element.17), channel_id=1, source_target_pairs={{1,2},{2,1},{5,6},{6,5}} | collective-permute-start | bytes 6291464 | tf_op jit(solution)/shard_map/ppermute | solution.py:794
  1382.4 92.2 %collective-permute-start.4 = (f32[3,128,2048]{2,1,0:T(8,128)}, f32[3,128,2048]{2,1,0:T(8,128)}, u32[]{:S(2)}, u32[]{:S(2)}) collective-permute-start(f32[3,128,2048]{2,1,0:T(8,128)} %collective-permute-done.refs_1_), channel_id=1, source_target_pairs={{1,5},{5,1},{2,6},{6,2}} | collective-permute-start | bytes 9437192 | tf_op jit(solution)/shard_map/ppermute | solution.py:793
  1416.1 63.2 %collective-permute-start.6 = (f32[3,128,2048]{2,1,0:T(8,128)}, f32[3,128,2048]{2,1,0:T(8,128)}, u32[]{:S(2)}, u32[]{:S(2)}) collective-permute-start(f32[3,128,2048]{2,1,0:T(8,128)} %collective-permute-done.1.refs_1_), channel_id=1, source_target_pairs={{1,5},{5,1},{2,6},{6,2}} | collective-permute-start | bytes 9437192 | tf_op jit(solution)/shard_map/ppermute | solution.py:793
  1462.5 27.7 %collective-permute-start.7 = (f32[2,128,2048]{2,1,0:T(8,128)}, f32[2,128,2048]{2,1,0:T(8,128)}, u32[]{:S(2)}, u32[]{:S(2)}) collective-permute-start(f32[2,128,2048]{2,1,0:T(8,128)} %get-tuple-element.18), channel_id=1, source_target_pairs={{1,2},{2,1},{5,6},{6,5}} | collective-permute-start | bytes 6291464 | tf_op jit(solution)/shard_map/ppermute | solution.py:794
  1466.1 27.1 %collective-permute-start.8 = (f32[2,128,2048]{2,1,0:T(8,128)}, f32[2,128,2048]{2,1,0:T(8,128)}, u32[]{:S(2)}, u32[]{:S(2)}) collective-permute-start(f32[2,128,2048]{2,1,0:T(8,128)} %collective-permute-done.3.refs_1_), channel_id=1, source_target_pairs={{1,5},{5,1},{2,6},{6,2}} | collective-permute-start | bytes 6291464 | tf_op jit(solution)/shard_map/ppermute | solution.py:793

commit v4 on v3

--- a/solution.py
+++ b/solution.py
@@ -10,6 +10,7 @@
 NT = (((1,), (1,)), ((), ()))
 F32 = jnp.float32
 
+SQUARE = 128
 TILE = 512
 CHUNK = 128
 STRIPS = 24
@@ -19,6 +20,10 @@
 WHOLE = 2
 INSIDE = 4
 PIECES = ((4, 8), (8, 11), (11, 14), (14, 16))
+
+
+def half_of(value):
+    return lax.rem(value, 2)
 
 
 def kernel(a, out, blk, prv, awy, pkl, pkr, late, *refs):
@@ -53,7 +58,7 @@
         pl.semaphore_wait(barrier, 7)
 
     def x_in(c):
-        part = lax.rem(g, 2)
+        part = half_of(g)
         return remote(a.at[1 - side, at(c * CHUNK, CHUNK)], blk.at[1 + part, at(c * CHUNK, CHUNK)],
                       s_x.at[c], r_x.at[part, c], y, 2 - side)
 
@@ -91,7 +96,7 @@
 
         def count(r):
             p, _, i = phase(r)
-            return (i + 1) + lax.rem(p, 2) * (n_strip - 1 - i)
+            return (i + 1) + half_of(p) * (n_strip - 1 - i)
 
         def slot(p):
             return p * (1 - 2 * d) + 2 * d
@@ -108,7 +113,7 @@
         def load_res(r, k):
             p, layer, i = phase(r)
             own = p + 1 - d < 2
-            load(own, layer, i * TILE, k * kc, kc, res.at[lax.rem(r, 2), :, at(k * kc, kc)], l_res.at[lax.rem(r, 2) * KSTEPS + k])
+            load(own, layer, i * TILE, k * kc, kc, res.at[half_of(r), :, at(k * kc, kc)], l_res.at[half_of(r) * KSTEPS + k])
 
         def load_stm(r, j, k):
             p, layer, _ = phase(r)
@@ -136,49 +141,53 @@
             p, layer, i = phase(r)
 
             def part(ref):
-                return ref.at[slot(p), layer, pl.ds(pl.multiple_of(i * TILE + row, 128), height), pl.ds(pl.multiple_of(j * TILE, TILE), width)]
+                return ref.at[slot(p), layer, pl.ds(pl.multiple_of(i * TILE + row, SQUARE), height), pl.ds(pl.multiple_of(j * TILE, TILE), width)]
 
             return remote(part(out), part(prv), s_y.at[lax.rem(r, 8) * 4 + j], r_y.at[r * 4 + j], 1 - y, g)
 
+        def packed_no(r):
+            return lax.rem(r, 8) + 8 * lax.div(phase(r)[0], 2)
+
         def packed(r):
-            e = lax.rem(r, 8) + 8 * lax.div(phase(r)[0], 2)
+            e = packed_no(r)
             return remote(pkl.at[e], pkr.at[e], s_y.at[32 + lax.rem(r, 8)], r_y.at[4 * STRIPS + e], 1 - y, g)
 
         def store_packed(r):
-            return pltpu.make_async_copy(pk, pkl.at[lax.rem(r, 8) + 8 * lax.div(phase(r)[0], 2)], l_pk.at[0])
+            return pltpu.make_async_copy(pk, pkl.at[packed_no(r)], l_pk.at[0])
 
         def load_packed(r):
-            e = lax.rem(r, 8) + 8 * lax.div(phase(r)[0], 2)
+            e = packed_no(r)
             return pltpu.make_async_copy(pkl.at[e], fpa, l_pk.at[1]), pltpu.make_async_copy(pkr.at[e], fpb, l_pk.at[2])
 
-        row_id = lax.broadcasted_iota(jnp.int32, (128, 128), 0)
-        col_id = lax.broadcasted_iota(jnp.int32, (128, 128), 1)
+        row_id = lax.broadcasted_iota(jnp.int32, (SQUARE, SQUARE), 0)
+        col_id = lax.broadcasted_iota(jnp.int32, (SQUARE, SQUARE), 1)
+
+        def square(ref, k):
+            span = pl.ds(SQUARE * k, SQUARE)
+            return ref.at[span, span]
 
         def pack(tile):
             ends = []
             for h in range(2):
-                one, two = 256 * h, 256 * h + 128
-                first = tile[pl.ds(one, 128), pl.ds(one, 128)]
-                second = tile[pl.ds(two, 128), pl.ds(two, 128)]
-                pk[pl.ds(128 * h, 128), :] = jnp.where(row_id > col_id, first, second.T)
+                first, second = square(tile, 2 * h)[...], square(tile, 2 * h + 1)[...]
+                pk[pl.ds(SQUARE * h, SQUARE), :] = jnp.where(row_id > col_id, first, second.T)
                 ends.append(jnp.sum(jnp.where(row_id == col_id, first, 0.0), axis=0, keepdims=True))
-            pk[pl.ds(256, 8), :] = jnp.where(row_id[:8] == 0, ends[0], ends[1])
+            pk[pl.ds(2 * SQUARE, 8), :] = jnp.where(row_id[:8] == 0, *ends)
 
         def unpack(tile):
             fpa[...] = fpa[...] + fpb[...]
             for h in range(2):
-                one, two = 256 * h, 256 * h + 128
-                both = fpa[pl.ds(128 * h, 128), :]
-                turned = both.T
-                ends = fpa[pl.ds(256 + h, 1), :]
-                tile[pl.ds(one, 128), pl.ds(one, 128)] = jnp.where(row_id > col_id, both, jnp.where(row_id == col_id, ends, turned))
-                tile[pl.ds(two, 128), pl.ds(two, 128)] = jnp.where(row_id <= col_id, both, turned)
+                shared = fpa[pl.ds(SQUARE * h, SQUARE), :]
+                turned = shared.T
+                ends = fpa[pl.ds(2 * SQUARE + h, 1), :]
+                square(tile, 2 * h)[...] = jnp.where(row_id > col_id, shared, jnp.where(row_id == col_id, ends, turned))
+                square(tile, 2 * h + 1)[...] = jnp.where(row_id <= col_id, shared, turned)
 
         def send(r, j):
             @pl.when(is_diag(r, j))
             def _():
-                for q in range(1, 4):
-                    lower(r, j, q * 128, 128, q * 128).start()
+                for row in range(SQUARE, TILE, SQUARE):
+                    lower(r, j, row, SQUARE, row).start()
                 store_packed(r).wait()
                 packed(r).start()
 
@@ -189,7 +198,7 @@
         def wait_exchange(r, j):
             @pl.when(is_diag(r, j))
             def _():
-                sized = lower(r, j, 0, 192, TILE)
+                sized = lower(r, j, 0, 3 * SQUARE // 2, TILE)
                 sized.wait_send()
                 sized.wait_recv()
                 packed(r).wait_send()
@@ -201,14 +210,14 @@
                 whole(r, j).wait_recv()
 
         def store_acc(r, j):
-            return pltpu.make_async_copy(acc.at[lax.rem(j, 2)], tile_of(out, r, phase(r)[2], j), l_acc.at[lax.rem(j, 2)])
+            return pltpu.make_async_copy(acc.at[half_of(j)], tile_of(out, r, phase(r)[2], j), l_acc.at[half_of(j)])
 
         def finish(r):
             n = count(r)
             i = phase(r)[2]
 
             def loads(j):
-                b = lax.rem(j, 2)
+                b = half_of(j)
                 return (pltpu.make_async_copy(tile_of(out, r, i, j), fa.at[b], l_fa.at[b]),
                         pltpu.make_async_copy(tile_of(prv, r, i, j), fb.at[b], l_fb.at[b]))
 
@@ -223,10 +232,10 @@
                         copy.start()
 
             def main_store(j):
-                return pltpu.make_async_copy(fa.at[lax.rem(j, 2)], tile_of(out, r, i, j), l_st.at[lax.rem(j, 2)])
+                return pltpu.make_async_copy(fa.at[half_of(j)], tile_of(out, r, i, j), l_st.at[half_of(j)])
 
             def mirror_store(j):
-                return pltpu.make_async_copy(fc.at[lax.rem(j, 2)], tile_of(out, r, j, i), l_tr.at[lax.rem(j, 2)])
+                return pltpu.make_async_copy(fc.at[half_of(j)], tile_of(out, r, j, i), l_tr.at[half_of(j)])
 
             def wait_stores(j):
                 main_store(j).wait()
@@ -238,7 +247,7 @@
             start_loads(0)
 
             def one(j, carry):
-                b = lax.rem(j, 2)
+                b = half_of(j)
 
                 @pl.when(j + 1 < n)
                 def _():
@@ -309,7 +318,7 @@
                 def before(k):
                     @pl.when(j == 0)
                     def _():
-                        b = lax.rem(r, 2)
+                        b = half_of(r)
                         pltpu.make_async_copy(a.at[0, pl.ds(0, TILE), pl.ds(0, kc)], res.at[b, :, pl.ds(0, kc)], l_res.at[b * KSTEPS + k]).wait()
 
                 def after(k):
@@ -326,12 +335,12 @@
                         store_acc(r, j - 1).wait()
                         send(r, j - 1)
 
-                body_steps(res.at[lax.rem(r, 2)], acc.at[lax.rem(j, 2)], False, before, after)
+                body_steps(res.at[half_of(r)], acc.at[half_of(j)], False, before, after)
                 store_acc(r, j).start()
 
                 @pl.when(is_diag(r, j))
                 def _():
-                    pack(acc.at[lax.rem(j, 2)])
+                    pack(acc.at[half_of(j)])
                     store_packed(r).start()
 
                 @pl.when(jnp.logical_and(r == 0, j == 0))
@@ -394,15 +403,15 @@
                 pltpu.make_async_copy(blk.at[0, at(js * TILE, TILE), at(k * kc, kc)], stm.at[k], l_stm.at[k]).start()
 
         def res_copy(c, part):
-            b = lax.rem(c, 2)
+            b = half_of(c)
             return pltpu.make_async_copy(blk.at[1 + part, at(c * CHUNK, CHUNK)], res.at[b, pl.ds(part * CHUNK, CHUNK)], l_fb.at[part])
 
         def acc_view(t):
-            b = lax.rem(t, 2)
+            b = half_of(t)
             return acc.at[b, pl.ds(0, 2 * CHUNK), :] if is_left else acc.at[b, :, pl.ds(0, 2 * CHUNK)]
 
         def store_acc(c, t):
-            b, half, js = lax.rem(t, 2), lax.div(t, 4), lax.rem(t, 4)
+            b, half, js = half_of(t), lax.div(t, 4), lax.rem(t, 4)
 
             def views(q, dst):
                 src = acc.at[b, pl.ds(q * CHUNK, CHUNK), :] if is_left else acc.at[b, :, pl.ds(q * CHUNK, CHUNK)]
@@ -565,11 +574,11 @@
                         def _():
                             send_half(0 * t)
 
-                        @pl.when(jnp.logical_and(c == n_chunk - 1, jnp.logical_and(lax.rem(t, 3) == 2, t < 3 * (INSIDE - WHOLE))))
+                        @pl.when(jnp.logical_and(c == n_chunk - 1, lax.rem(t, 3) == 2))
                         def _():
                             forward(WHOLE + lax.div(t, 3))
 
-                body_steps(res.at[lax.rem(c, 2), pl.ds(0, 2 * CHUNK), :], acc_view(t), not is_left, lambda k: None, after)
+                body_steps(res.at[half_of(c), pl.ds(0, 2 * CHUNK), :], acc_view(t), not is_left, lambda k: None, after)
                 store_acc(c, t)(lambda copy: copy.start())
                 return carry
 
@@ -757,8 +766,7 @@
                 jax.ShapeDtypeStruct((3, rows, cols), a_loc.dtype),
                 slots_shape,
                 jax.ShapeDtypeStruct((2, rows, rows), F32),
-                jax.ShapeDtypeStruct((16, PACKED, 128), F32),
-                jax.ShapeDtypeStruct((16, PACKED, 128), F32),
+                *(jax.ShapeDtypeStruct((16, PACKED, SQUARE), F32) for _ in range(2)),
                 chunks_shape(PIECES[0][1] - PIECES[0][0]),
                 *(chunks_shape(2) for _ in range(WHOLE)),
                 *(chunks_shape(stop - start) for start, stop in PIECES),
@@ -768,16 +776,11 @@
             scratch_shapes=[
                 pltpu.VMEM((2, TILE, cols), a_loc.dtype),
                 pltpu.VMEM((KSTEPS, TILE, cols // KSTEPS), a_loc.dtype),
-                pltpu.VMEM((2, TILE, TILE), F32),
-                pltpu.VMEM((2, TILE, TILE), F32),
-                pltpu.VMEM((2, TILE, TILE), F32),
-                pltpu.VMEM((2, TILE, TILE), F32),
-                pltpu.VMEM((PACKED, 128), F32),
-                pltpu.VMEM((PACKED, 128), F32),
-                pltpu.VMEM((PACKED, 128), F32),
+                *[pltpu.VMEM((2, TILE, TILE), F32)] * 4,
+                *[pltpu.VMEM((PACKED, SQUARE), F32)] * 3,
                 dma((n_chunk,)), dma((2, n_chunk)), dma((2,)), dma((2,)),
                 dma((4 * n_chunk,)), dma((4 * STRIPS + 16,)), dma((n_chunk,)), dma((n_chunk,)),
-                dma((2 * KSTEPS,)), dma((KSTEPS,)), dma((4,)), dma((4,)), dma((4,)), dma((4,)), dma((2,)), dma((3,)),
+                dma((2 * KSTEPS,)), dma((KSTEPS,)), *[dma((4,))] * 6,
             ],
             compiler_params=pltpu.CompilerParams(
                 collective_id=0, has_side_effects=True, vmem_limit_bytes=63 * 2**20),
@@ -823,12 +826,10 @@
             )(*operands)
 
         result = assemble(0, None, [])
-        result = assemble(1, result, [("mine", 0)])
-        result = assemble(2, result, [("mine", 1)])
-        result = assemble(3, result, [("mine", 2), ("theirs", 0)])
-        result = assemble(4, result, [("mine", 3), ("theirs", 1)])
-        result = assemble(5, result, [("pair", 0), ("theirs", 2)])
-        result = assemble(6, result, [("pair", 1), ("theirs", 3)])
+        for step in range(1, n_pieces + WHOLE + 1):
+            own, other = step - 1, step - WHOLE - 1
+            parts = [("mine", own) if own < n_pieces else ("pair", own - n_pieces)]
+            result = assemble(step, result, parts + ([("theirs", other)] if other >= 0 else []))
         return result[None]
 
     return jax.shard_map(local_part, mesh=mesh, in_specs=(P(None, ("m", "g"), "kk"),),

time: 1500 us -> 1500 us (level)
  no operation moved by 1% of the time
where the time goes in v4:
time: 1500 us
  Pallas kernels  1410 us (94%)
  waiting for transfers between devices  56.7 us (4%)
  starting transfers between devices  27.8 us (2%)
    pallas_call x1, Pallas kernels, local_part(): pl.pallas_call(kernel, out_shape=(slots_shape, jax.ShapeDtypeStruct((3, r...  1340 us
    pallas_call x7, Pallas kernels, assemble(): pl.pallas_call(body, out_shape=slots_shape, in_specs=[any_space] * len(op...  68.9 us
    ppermute x3, waiting for transfers between devices, local_part(): lax.ppermute(pieces[k], 'g', other_chip)  47.4 us
  transfers between devices with their start and end apart: 9, of which 4 were waited for; matrix products, arithmetic and copies ran while one was open for 0% of the time, Pallas kernels for 4%

profile of v4, /device:TPU:1, one launch (start us, length us, event | category | flops | bytes accessed | tf_op | source)
XLA Modules:
  0.0 1496.9 jit_solution(4031393596283223057)
XLA Ops:
  0.0 1343.2 %shard_map.17 = (f32[3,2,2048,2048]{3,2,1,0:T(8,128)}, bf16[3,2048,14336]{2,1,0:T(8,128)(2,1)}, f32[3,2,2048,2048]{3,2,1,0:T(8,128)}, f32[2,2048,2048]{2,1,0:T(8...) custom-call(bf16[2,2048,14336]{2,1,0:T(8,128)(2,1)} %a.1), custom_call_target="tpu_custom_call" | custom-call | flops 999999995904 | bytes 1000000000 | tf_op jit(solution)/shard_map/pallas_call | solution.py:762
  1343.2 3.9 collective-permute-start
  1347.1 1.9 collective-permute-start.1
  1349.1 3.6 collective-permute-start.2
  1352.6 3.4 collective-permute-start.3
  1356.1 2.1 collective-permute-start.5
  1358.2 24.2 %collective-permute-done.refs_1_ = f32[3,128,2048]{2,1,0:T(8,128)} collective-permute-done((f32[3,128,2048]{2,1,0:T(8,128)}, f32[3,128,2048]{2,1,0:T(8,128)}, u32[]{:S(2)}, u32[]{:S(2)}) %collective-permute-start) | collective-permute-done | bytes 3145760 | tf_op jit(solution)/shard_map/ppermute | solution.py:795
  1382.4 3.5 collective-permute-start.4
  1386.0 6.9 shard_map.18.refs_0_
  1392.8 23.3 %collective-permute-done.1.refs_1_ = f32[3,128,2048]{2,1,0:T(8,128)} collective-permute-done((f32[3,128,2048]{2,1,0:T(8,128)}, f32[3,128,2048]{2,1,0:T(8,128)}, u32[]{:S(2)}, u32[]{:S(2)}) %collective-permute-start.1) | collective-permute-done | bytes 3145760 | tf_op jit(solution)/shard_map/ppermute | solution.py:795
  1416.1 3.5 collective-permute-start.6
  1419.7 15.7 %shard_map.19.refs_0_ = f32[3,2,2048,2048]{3,2,1,0:T(8,128)} custom-call(f32[3,2,2048,2048]{3,2,1,0:T(8,128)} %shard_map.18.refs_0_, f32[4,128,2048]{2,1,0:T(8,128)} %get-tuple-element.13.refs_1_, f32[3,2,2048,2048]{3,2,1,0:T(8,128)} %get-tuple-element.12.refs_0_.refs_2_), custom_call_target="tpu_custom_call", output_to_operand_aliasing={{}: (0, {})} | custom-call | flops 10000000000 | bytes 100000000 | tf_op jit(solution)/shard_map/pallas_call | solution.py:814
  1435.4 27.1 %shard_map.20.refs_0_ = f32[3,2,2048,2048]{3,2,1,0:T(8,128)} custom-call(f32[3,2,2048,2048]{3,2,1,0:T(8,128)} %shard_map.19.refs_0_, f32[3,128,2048]{2,1,0:T(8,128)} %collective-permute-done.refs_1_, f32[3,2,2048,2048]{3,2,1,0:T(8,128)} %get-tuple-element.12.refs_0_.refs_2_), custom_call_target="tpu_custom_call", output_to_operand_aliasing={{}: (0, {})} | custom-call | flops 10000000000 | bytes 100000000 | tf_op jit(solution)/shard_map/pallas_call | solution.py:814
  1462.5 0.0 collective-permute-done.3.refs_1_
  1462.5 3.5 collective-permute-start.7
  1466.1 0.0 collective-permute-done.2.refs_2_
  1466.1 2.2 collective-permute-start.8
  1468.3 6.3 shard_map.21.refs_0_
  1474.6 0.0 collective-permute-done.4.refs_2_
  1474.6 4.6 shard_map.22.refs_0_
  1479.3 0.0 collective-permute-done.5.refs_1_
  1479.3 0.0 collective-permute-done.6.refs_2_
  1479.3 4.6 shard_map.23.refs_0_
  1484.0 6.2 collective-permute-done.7.refs_1_
  1490.2 3.0 collective-permute-done.8.refs_2_
  1493.2 3.5 shard_map.24
Async XLA Ops:
  1343.2 39.2 %collective-permute-start = (f32[3,128,2048]{2,1,0:T(8,128)}, f32[3,128,2048]{2,1,0:T(8,128)}, u32[]{:S(2)}, u32[]{:S(2)}) collective-permute-start(f32[3,128,2048]{2,1,0:T(8,128)} %get-tuple-element.14), channel_id=1, source_target_pairs={{1,2},{2,1},{5,6},{6,5}} | collective-permute-start | bytes 9437192 | tf_op jit(solution)/shard_map/ppermute | solution.py:795
  1347.1 69.0 %collective-permute-start.1 = (f32[3,128,2048]{2,1,0:T(8,128)}, f32[3,128,2048]{2,1,0:T(8,128)}, u32[]{:S(2)}, u32[]{:S(2)}) collective-permute-start(f32[3,128,2048]{2,1,0:T(8,128)} %get-tuple-element.15), channel_id=1, source_target_pairs={{1,2},{2,1},{5,6},{6,5}} | collective-permute-start | bytes 9437192 | tf_op jit(solution)/shard_map/ppermute | solution.py:795
  1349.1 117.0 %collective-permute-start.2 = (f32[4,128,2048]{2,1,0:T(8,128)}, f32[4,128,2048]{2,1,0:T(8,128)}, u32[]{:S(2)}, u32[]{:S(2)}) collective-permute-start(f32[4,128,2048]{2,1,0:T(8,128)} %get-tuple-element.13.refs_1_), channel_id=1, source_target_pairs={{1,5},{5,1},{2,6},{6,2}} | collective-permute-start | bytes 12582920 | tf_op jit(solution)/shard_map/ppermute | solution.py:796
  1352.6 109.9 %collective-permute-start.3 = (f32[2,128,2048]{2,1,0:T(8,128)}, f32[2,128,2048]{2,1,0:T(8,128)}, u32[]{:S(2)}, u32[]{:S(2)}) collective-permute-start(f32[2,128,2048]{2,1,0:T(8,128)} %get-tuple-element.16), channel_id=1, source_target_pairs={{1,2},{2,1},{5,6},{6,5}} | collective-permute-start | bytes 6291464 | tf_op jit(solution)/shard_map/ppermute | solution.py:795
  1356.1 123.2 %collective-permute-start.5 = (f32[2,128,2048]{2,1,0:T(8,128)}, f32[2,128,2048]{2,1,0:T(8,128)}, u32[]{:S(2)}, u32[]{:S(2)}) collective-permute-start(f32[2,128,2048]{2,1,0:T(8,128)} %get-tuple-element.17), channel_id=1, source_target_pairs={{1,2},{2,1},{5,6},{6,5}} | collective-permute-start | bytes 6291464 | tf_op jit(solution)/shard_map/ppermute | solution.py:797
  1382.4 92.2 %collective-permute-start.4 = (f32[3,128,2048]{2,1,0:T(8,128)}, f32[3,128,2048]{2,1,0:T(8,128)}, u32[]{:S(2)}, u32[]{:S(2)}) collective-permute-start(f32[3,128,2048]{2,1,0:T(8,128)} %collective-permute-done.refs_1_), channel_id=1, source_target_pairs={{1,5},{5,1},{2,6},{6,2}} | collective-permute-start | bytes 9437192 | tf_op jit(solution)/shard_map/ppermute | solution.py:796
  1416.1 63.2 %collective-permute-start.6 = (f32[3,128,2048]{2,1,0:T(8,128)}, f32[3,128,2048]{2,1,0:T(8,128)}, u32[]{:S(2)}, u32[]{:S(2)}) collective-permute-start(f32[3,128,2048]{2,1,0:T(8,128)} %collective-permute-done.1.refs_1_), channel_id=1, source_target_pairs={{1,5},{5,1},{2,6},{6,2}} | collective-permute-start | bytes 9437192 | tf_op jit(solution)/shard_map/ppermute | solution.py:796
  1462.5 27.7 %collective-permute-start.7 = (f32[2,128,2048]{2,1,0:T(8,128)}, f32[2,128,2048]{2,1,0:T(8,128)}, u32[]{:S(2)}, u32[]{:S(2)}) collective-permute-start(f32[2,128,2048]{2,1,0:T(8,128)} %get-tuple-element.18), channel_id=1, source_target_pairs={{1,2},{2,1},{5,6},{6,5}} | collective-permute-start | bytes 6291464 | tf_op jit(solution)/shard_map/ppermute | solution.py:797
  1466.1 27.1 %collective-permute-start.8 = (f32[2,128,2048]{2,1,0:T(8,128)}, f32[2,128,2048]{2,1,0:T(8,128)}, u32[]{:S(2)}, u32[]{:S(2)}) collective-permute-start(f32[2,128,2048]{2,1,0:T(8,128)} %collective-permute-done.3.refs_1_), channel_id=1, source_target_pairs={{1,5},{5,1},{2,6},{6,2}} | collective-permute-start | bytes 6291464 | tf_op jit(solution)/shard_map/ppermute | solution.py:796

commit v5 on v4

--- a/solution.py
+++ b/solution.py
@@ -49,13 +49,11 @@
     def remote(src, dst, ss, rs, kk2, g2):
         return pltpu.make_async_remote_copy(src, dst, ss, rs, device_id=(m, kk2, g2), device_id_type=MESH)
 
-    def enter():
+    def enter(*peers):
         barrier = pltpu.get_barrier_semaphore()
-        me = y * 4 + g
-        for step in range(1, 8):
-            other = lax.rem(me + step, 8)
-            pl.semaphore_signal(barrier, inc=1, device_id=(m, lax.div(other, 4), lax.rem(other, 4)), device_id_type=MESH)
-        pl.semaphore_wait(barrier, 7)
+        for peer in ((1 - y, g),) + peers:
+            pl.semaphore_signal(barrier, inc=1, device_id=(m,) + peer, device_id_type=MESH)
+        pl.semaphore_wait(barrier, 1 + len(peers))
 
     def x_in(c):
         part = half_of(g)
@@ -289,7 +287,7 @@
 
         load_res(0, 0)
         load_stm(0, 0, 0)
-        enter()
+        enter((y, mate), (y, 2 - side))
         lax.fori_loop(0, n_chunk, x_start, 0)
         for k in range(1, KSTEPS):
             load_res(0, k)
@@ -369,7 +367,7 @@
         lc = 0 if is_left else 1
         mate = 0 if is_left else 3
         partner = 2 if is_left else 1
-        enter()
+        enter((y, mate), (y, partner), (y, 3 - mate))
         lax.fori_loop(0, n_chunk, x_start, 0)
         for layer in range(layers):
             remote(a.at[layer], blk.at[layer], s_d.at[layer], r_d.at[layer], y, mate).start()
@@ -392,7 +390,7 @@
 
         def load_stm(t, k):
             half, js = lax.div(t, 4), lax.rem(t, 4)
-            own = block_of(half) == 1 if is_left else half == 1
+            own = block_of(half) == 1 if is_left else half == 0
 
             @pl.when(own)
             def _():
@@ -424,12 +422,12 @@
                 @pl.when(half == 0)
                 def _():
                     for q in range(2):
+                        op(views(q, out.at[q, lc]))
+
+                @pl.when(half == 1)
+                def _():
+                    for q in range(2):
                         op(views(q, awy.at[kept(q)]))
-
-                @pl.when(half == 1)
-                def _():
-                    for q in range(2):
-                        op(views(q, out.at[q, lc]))
 
             return both
 
@@ -551,12 +549,12 @@
                 else:
                     @pl.when(half == 0)
                     def _():
-                        spread(c).start()
-
-                    @pl.when(half == 1)
-                    def _():
                         for b in range(2):
                             home(c, b).start()
+
+                    @pl.when(half == 1)
+                    def _():
+                        spread(c).start()
 
             def tile(t, carry):
                 last = lax.div(t + 1, 8)
@@ -574,9 +572,9 @@
                         def _():
                             send_half(0 * t)
 
-                        @pl.when(jnp.logical_and(c == n_chunk - 1, lax.rem(t, 3) == 2))
+                        @pl.when(jnp.logical_and(c == n_chunk - 1, t == 2))
                         def _():
-                            forward(WHOLE + lax.div(t, 3))
+                            forward(WHOLE)
 
                 body_steps(res.at[half_of(c), pl.ds(0, 2 * CHUNK), :], acc_view(t), not is_left, lambda k: None, after)
                 store_acc(c, t)(lambda copy: copy.start())
@@ -586,7 +584,28 @@
             store_acc(c, 7)(lambda copy: copy.wait())
             send_half(1 + 0 * c)
 
+            @pl.when(c == n_chunk - 1)
+            def _():
+                for k in range(WHOLE + 1, INSIDE):
+                    forward(k)
+
+        early = n_chunk - 2
+
+        def drain_early():
+            lax.fori_loop(0, early, x_wait_send, 0)
+            lax.fori_loop(0, early, drain_spread, 0)
+            for layer in range(layers):
+                remote(a.at[layer], blk.at[layer], s_d.at[layer], r_d.at[layer], y, mate).wait_send()
+            for k in range(WHOLE):
+                gather_here(k).wait_send()
+                gather_here(k).wait_recv()
+
+        def drain_spread(c, carry):
+            spread(c).wait_send()
+            return carry
+
         def chunk(c, carry):
+            pl.when(c == n_chunk - 1)(drain_early)
             compute(c)
 
             @pl.when(c >= 1)
@@ -606,21 +625,12 @@
             gather(c, 1 - y).wait_recv()
             return carry
 
-        def drain_spread(c, carry):
-            spread(c).wait_send()
-            return carry
-
-        for k in range(WHOLE):
-            gather_here(k).wait_send()
-            gather_here(k).wait_recv()
-        lax.fori_loop(WHOLE, INSIDE, drain, 0)
-        lax.fori_loop(0, n_chunk, drain_spread, 0)
+        lax.fori_loop(early, n_chunk, drain_spread, 0)
+        lax.fori_loop(early, n_chunk, x_wait_send, 0)
         for c in range(*PIECES[0]):
             away_late(c).wait_send()
             away_late(c).wait_recv()
-        for layer in range(layers):
-            remote(a.at[layer], blk.at[layer], s_d.at[layer], r_d.at[layer], y, mate).wait_send()
-        lax.fori_loop(0, n_chunk, x_wait_send, 0)
+        lax.fori_loop(WHOLE, INSIDE, drain, 0)
 
     pl.when(lax.rem(g, 3) == 0)(diagonal)
     pl.when(g == 1)(lambda: cross(True))

time: 1500 us -> 1500 us (level)
  no operation moved by 1% of the time
where the time goes in v5:
time: 1500 us; the launch traced here: 1490 us
  Pallas kernels  1410 us (94%)
  waiting for transfers between devices  58.4 us (4%)
  starting transfers between devices  26.8 us (2%)
    pallas_call x1, Pallas kernels, local_part(): pl.pallas_call(kernel, out_shape=(slots_shape, jax.ShapeDtypeStruct((3, r...  1340 us
    pallas_call x7, Pallas kernels, assemble(): pl.pallas_call(body, out_shape=slots_shape, in_specs=[any_space] * len(op...  68.7 us
    ppermute x3, waiting for transfers between devices, local_part(): lax.ppermute(pieces[k], 'g', other_chip)  50.1 us
  transfers between devices with their start and end apart: 9, of which 4 were waited for; matrix products, arithmetic and copies ran while one was open for 0% of the time, Pallas kernels for 4%

profile of v5, /device:TPU:1, one launch (start us, length us, event | category | flops | bytes accessed | tf_op | source)
XLA Modules:
  0.0 1493.1 jit_solution(140771072310626983)
XLA Ops:
  0.0 1339.0 %shard_map.17 = (f32[3,2,2048,2048]{3,2,1,0:T(8,128)}, bf16[3,2048,14336]{2,1,0:T(8,128)(2,1)}, f32[3,2,2048,2048]{3,2,1,0:T(8,128)}, f32[2,2048,2048]{2,1,0:T(8...) custom-call(bf16[2,2048,14336]{2,1,0:T(8,128)(2,1)} %a.1), custom_call_target="tpu_custom_call" | custom-call | flops 999999995904 | bytes 1000000000 | tf_op jit(solution)/shard_map/pallas_call | solution.py:772
  1339.0 5.4 collective-permute-start
  1344.4 1.9 collective-permute-start.1
  1346.3 2.2 collective-permute-start.2
  1348.5 3.9 collective-permute-start.3
  1352.5 1.9 collective-permute-start.5
  1354.4 25.3 %collective-permute-done.refs_1_ = f32[3,128,2048]{2,1,0:T(8,128)} collective-permute-done((f32[3,128,2048]{2,1,0:T(8,128)}, f32[3,128,2048]{2,1,0:T(8,128)}, u32[]{:S(2)}, u32[]{:S(2)}) %collective-permute-start) | collective-permute-done | bytes 3145760 | tf_op jit(solution)/shard_map/ppermute | solution.py:805
  1379.7 2.2 collective-permute-start.4
  1381.9 6.7 shard_map.18.refs_0_
  1388.6 24.8 %collective-permute-done.1.refs_1_ = f32[3,128,2048]{2,1,0:T(8,128)} collective-permute-done((f32[3,128,2048]{2,1,0:T(8,128)}, f32[3,128,2048]{2,1,0:T(8,128)}, u32[]{:S(2)}, u32[]{:S(2)}) %collective-permute-start.1) | collective-permute-done | bytes 3145760 | tf_op jit(solution)/shard_map/ppermute | solution.py:805
  1413.4 2.2 collective-permute-start.6
  1415.6 15.7 %shard_map.19.refs_0_ = f32[3,2,2048,2048]{3,2,1,0:T(8,128)} custom-call(f32[3,2,2048,2048]{3,2,1,0:T(8,128)} %shard_map.18.refs_0_, f32[4,128,2048]{2,1,0:T(8,128)} %get-tuple-element.13.refs_1_, f32[3,2,2048,2048]{3,2,1,0:T(8,128)} %get-tuple-element.12.refs_0_.refs_2_), custom_call_target="tpu_custom_call", output_to_operand_aliasing={{}: (0, {})} | custom-call | flops 10000000000 | bytes 100000000 | tf_op jit(solution)/shard_map/pallas_call | solution.py:824
  1431.3 27.1 %shard_map.20.refs_0_ = f32[3,2,2048,2048]{3,2,1,0:T(8,128)} custom-call(f32[3,2,2048,2048]{3,2,1,0:T(8,128)} %shard_map.19.refs_0_, f32[3,128,2048]{2,1,0:T(8,128)} %collective-permute-done.refs_1_, f32[3,2,2048,2048]{3,2,1,0:T(8,128)} %get-tuple-element.12.refs_0_.refs_2_), custom_call_target="tpu_custom_call", output_to_operand_aliasing={{}: (0, {})} | custom-call | flops 10000000000 | bytes 100000000 | tf_op jit(solution)/shard_map/pallas_call | solution.py:824
  1458.4 0.0 collective-permute-done.3.refs_1_
  1458.4 4.0 collective-permute-start.7
  1462.4 0.0 collective-permute-done.2.refs_2_
  1462.4 3.1 collective-permute-start.8
  1465.5 6.3 shard_map.21.refs_0_
  1471.9 0.0 collective-permute-done.4.refs_2_
  1471.9 4.6 shard_map.22.refs_0_
  1476.5 0.0 collective-permute-done.5.refs_1_
  1476.6 0.0 collective-permute-done.6.refs_2_
  1476.6 4.6 shard_map.23.refs_0_
  1481.2 5.2 collective-permute-done.7.refs_1_
  1486.5 3.1 collective-permute-done.8.refs_2_
  1489.5 3.5 shard_map.24
Async XLA Ops:
  1339.0 40.6 %collective-permute-start = (f32[3,128,2048]{2,1,0:T(8,128)}, f32[3,128,2048]{2,1,0:T(8,128)}, u32[]{:S(2)}, u32[]{:S(2)}) collective-permute-start(f32[3,128,2048]{2,1,0:T(8,128)} %get-tuple-element.14), channel_id=1, source_target_pairs={{1,2},{2,1},{5,6},{6,5}} | collective-permute-start | bytes 9437192 | tf_op jit(solution)/shard_map/ppermute | solution.py:805
  1344.4 69.0 %collective-permute-start.1 = (f32[3,128,2048]{2,1,0:T(8,128)}, f32[3,128,2048]{2,1,0:T(8,128)}, u32[]{:S(2)}, u32[]{:S(2)}) collective-permute-start(f32[3,128,2048]{2,1,0:T(8,128)} %get-tuple-element.15), channel_id=1, source_target_pairs={{1,2},{2,1},{5,6},{6,5}} | collective-permute-start | bytes 9437192 | tf_op jit(solution)/shard_map/ppermute | solution.py:805
  1346.3 116.1 %collective-permute-start.2 = (f32[4,128,2048]{2,1,0:T(8,128)}, f32[4,128,2048]{2,1,0:T(8,128)}, u32[]{:S(2)}, u32[]{:S(2)}) collective-permute-start(f32[4,128,2048]{2,1,0:T(8,128)} %get-tuple-element.13.refs_1_), channel_id=1, source_target_pairs={{1,5},{5,1},{2,6},{6,2}} | collective-permute-start | bytes 12582920 | tf_op jit(solution)/shard_map/ppermute | solution.py:806
  1348.5 109.9 %collective-permute-start.3 = (f32[2,128,2048]{2,1,0:T(8,128)}, f32[2,128,2048]{2,1,0:T(8,128)}, u32[]{:S(2)}, u32[]{:S(2)}) collective-permute-start(f32[2,128,2048]{2,1,0:T(8,128)} %get-tuple-element.16), channel_id=1, source_target_pairs={{1,2},{2,1},{5,6},{6,5}} | collective-permute-start | bytes 6291464 | tf_op jit(solution)/shard_map/ppermute | solution.py:805
  1352.5 124.1 %collective-permute-start.5 = (f32[2,128,2048]{2,1,0:T(8,128)}, f32[2,128,2048]{2,1,0:T(8,128)}, u32[]{:S(2)}, u32[]{:S(2)}) collective-permute-start(f32[2,128,2048]{2,1,0:T(8,128)} %get-tuple-element.17), channel_id=1, source_target_pairs={{1,2},{2,1},{5,6},{6,5}} | collective-permute-start | bytes 6291464 | tf_op jit(solution)/shard_map/ppermute | solution.py:807
  1379.7 92.2 %collective-permute-start.4 = (f32[3,128,2048]{2,1,0:T(8,128)}, f32[3,128,2048]{2,1,0:T(8,128)}, u32[]{:S(2)}, u32[]{:S(2)}) collective-permute-start(f32[3,128,2048]{2,1,0:T(8,128)} %collective-permute-done.refs_1_), channel_id=1, source_target_pairs={{1,5},{5,1},{2,6},{6,2}} | collective-permute-start | bytes 9437192 | tf_op jit(solution)/shard_map/ppermute | solution.py:806
  1413.4 63.2 %collective-permute-start.6 = (f32[3,128,2048]{2,1,0:T(8,128)}, f32[3,128,2048]{2,1,0:T(8,128)}, u32[]{:S(2)}, u32[]{:S(2)}) collective-permute-start(f32[3,128,2048]{2,1,0:T(8,128)} %collective-permute-done.1.refs_1_), channel_id=1, source_target_pairs={{1,5},{5,1},{2,6},{6,2}} | collective-permute-start | bytes 9437192 | tf_op jit(solution)/shard_map/ppermute | solution.py:806
  1458.4 28.0 %collective-permute-start.7 = (f32[2,128,2048]{2,1,0:T(8,128)}, f32[2,128,2048]{2,1,0:T(8,128)}, u32[]{:S(2)}, u32[]{:S(2)}) collective-permute-start(f32[2,128,2048]{2,1,0:T(8,128)} %get-tuple-element.18), channel_id=1, source_target_pairs={{1,2},{2,1},{5,6},{6,5}} | collective-permute-start | bytes 6291464 | tf_op jit(solution)/shard_map/ppermute | solution.py:807
  1462.4 27.1 %collective-permute-start.8 = (f32[2,128,2048]{2,1,0:T(8,128)}, f32[2,128,2048]{2,1,0:T(8,128)}, u32[]{:S(2)}, u32[]{:S(2)}) collective-permute-start(f32[2,128,2048]{2,1,0:T(8,128)} %collective-permute-done.3.refs_1_), channel_id=1, source_target_pairs={{1,5},{5,1},{2,6},{6,2}} | collective-permute-start | bytes 6291464 | tf_op jit(solution)/shard_map/ppermute | solution.py:806
